TPU v7x, 256 devices: a whole 4x4x8 slice. The times are simulated.
256 devices in a mesh: vox: 32 (over x, z), frm: 8 (over y, core).
Axes of the slice: x: 4, y: 4, z: 8, core: 2. Of those that a mesh axis runs over, the one named last changes fastest.
Arguments:
- casorati: float32 [256, 1048576], P('frm', 'vox'), may hold values from -6 to 6
- start_vectors: float32 [256, 64], replicated, may hold values from -6 to 6
Outputs:
- vectors: float32 [256, 64], replicated
- filtered: float32 [256, 1048576], P('frm', 'vox')
All inputs are finite; a program needn't handle non-finite values.
Results may differ from a plain program's by a relative error of at most 0.0003.
Values sent between devices are 32-bit elements; how exact they have to be, the bound alone decides.
No kernel may reach another device: no remote copies, remote signals or barrier semaphores. Data moves between devices by JAX's collectives and lax.ppermute only.
A program may use at most 64 MiB of HBM per device.

v0:
```python
import jax
import jax.numpy as jnp
from jax import lax
from jax.sharding import PartitionSpec as P

ITERS = 3


def orthonormal(projected):
    small = jnp.dot(projected.T, projected, precision=lax.Precision.HIGHEST)
    lower = jnp.linalg.cholesky(small)
    return jax.scipy.linalg.solve_triangular(lower, projected.T, lower=True).T


def contract_cols(left, right):
    return lax.dot_general(left, right, (((1,), (1,)), ((), ())), precision=lax.Precision.HIGHEST)


def body(casorati, start_vectors):
    high = lax.Precision.HIGHEST
    columns = lax.all_to_all(casorati, "frm", split_axis=1, concat_axis=0, tiled=True)
    vectors = start_vectors
    gram = lax.psum(contract_cols(columns, columns), ("vox", "frm"))
    for step in range(ITERS):
        vectors = orthonormal(jnp.dot(gram, vectors, precision=high))
    image = jnp.dot(vectors.T, columns, precision=high)
    cleaned = columns - jnp.dot(vectors, image, precision=high)
    filtered = lax.all_to_all(cleaned, "frm", split_axis=0, concat_axis=1, tiled=True)
    return (vectors, filtered)


def solution(mesh):
    return jax.shard_map(
        body,
        mesh=mesh,
        in_specs=(P("frm", "vox"), P()),
        out_specs=(P(), P("frm", "vox")),
        check_vma=False,
    )
```

profile of v0, /device:TPU:1, one launch (start us, length us, event | category | flops | bytes accessed | tf_op | source)
XLA Modules:
  0.0 439.2 jit_solution(6300421162435829649)
XLA Ops:
  7.2 0.0 copy-start
  7.2 0.0 all-reduce.2.cloned.1.call-start
  7.2 2.5 copy.12
  9.7 54.4 %all_to_all.38 = f32[32,8,4096]{2,0,1:T(8,128)S(1)} all-to-all(f32[32,8,4096]{2,0,1:T(8,128)S(1)} %bitcast.71), channel_id=1, replica_groups=mesh['vox'=32,'frm'=8] {'frm'}, dimensions={1} | all-to-all | bytes 8388608 | tf_op jit(solution)/shard_map/all_to_all | solution.py:21
  64.1 0.0 copy-start.1
  64.1 2.0 copy-done.1
  66.1 4.2 fusion.19
  70.4 0.0 all-reduce.2.cloned.1.call-update
  70.4 254.1 %all-reduce.2.cloned.1.call-done = f32[256,256]{1,0:T(8,128)} async-done(((f32[256,256]{1,0:T(8,128)}), f32[256,256]{1,0:T(8,128)}) %all-reduce.2.cloned.1.call-update) | async-done | bytes 262160 | tf_op jit(solution)/shard_map/psum | solution.py:23
  324.5 0.0 copy-done
  324.5 1.3 fusion.20
  325.8 0.2 fusion.21
  326.0 0.1 copy.5
  326.1 5.8 %cholesky.59 = f32[64,64]{1,0:T(8,128)S(1)} custom-call(f32[64,64]{1,0:T(8,128)S(1)} %fusion.14), custom_call_target="Cholesky" | custom-call | tf_op jit(solution)/shard_map/jit(cholesky)/cholesky | solution.py:11
  332.0 0.6 compare_reduce_fusion.2
  332.7 0.7 fusion.6
  333.3 4.9 %custom-call.7 = f32[1,64,64]{1,2,0:T(8,128)S(1)} custom-call(f32[1,64,64]{2,1,0:T(8,128)S(1)} %fusion.6), custom_call_target="InvertDiagBlocksLowerTriangular" | custom-call | tf_op jit(solution)/shard_map/jit(_solve_triangular)/triangular_solve | solution.py:12
  338.2 0.3 fusion.4
  338.5 1.3 fusion.22
  339.8 0.2 fusion.23
  340.0 0.1 copy.6
  340.1 5.8 %cholesky.70 = f32[64,64]{1,0:T(8,128)S(1)} custom-call(f32[64,64]{1,0:T(8,128)S(1)} %fusion.12), custom_call_target="Cholesky" | custom-call | tf_op jit(solution)/shard_map/jit(cholesky)/cholesky | solution.py:11
  346.0 0.6 compare_reduce_fusion.1
  346.7 0.7 fusion.7
  347.3 4.9 %custom-call.8 = f32[1,64,64]{1,2,0:T(8,128)S(1)} custom-call(f32[1,64,64]{2,1,0:T(8,128)S(1)} %fusion.7), custom_call_target="InvertDiagBlocksLowerTriangular" | custom-call | tf_op jit(solution)/shard_map/jit(_solve_triangular)/triangular_solve | solution.py:12
  352.2 0.3 fusion.2
  352.5 1.3 fusion.24
  353.8 0.2 fusion.25
  354.0 0.1 copy.7
  354.1 5.8 %cholesky.81 = f32[64,64]{1,0:T(8,128)S(1)} custom-call(f32[64,64]{1,0:T(8,128)S(1)} %fusion.10), custom_call_target="Cholesky" | custom-call | tf_op jit(solution)/shard_map/jit(cholesky)/cholesky | solution.py:11
  360.0 0.6 compare_reduce_fusion
  360.6 0.7 fusion.8
  361.3 4.9 %custom-call.9 = f32[1,64,64]{1,2,0:T(8,128)S(1)} custom-call(f32[1,64,64]{2,1,0:T(8,128)S(1)} %fusion.8), custom_call_target="InvertDiagBlocksLowerTriangular" | custom-call | tf_op jit(solution)/shard_map/jit(_solve_triangular)/triangular_solve | solution.py:12
  366.2 0.0 copy-start.2
  366.2 0.3 fusion
  366.5 0.0 copy-start.3
  366.5 5.2 %fusion.26 = f32[64,4096]{1,0:T(8,128)S(1)} fusion(f32[64,256]{1,0:T(8,128)S(1)} %fusion, f32[256,4096]{1,0:T(8,128)} %bitcast.67), kind=kOutput, calls=%fused_computation.40 | convolution fusion | flops 805306368 | bytes 5308416 | tf_op jit(solution)/shard_map/dot_general | solution.py:26
  371.7 0.0 copy-done.2
  371.7 3.5 convolution_subtract_fusion
  375.2 0.0 copy-done.3
  375.2 54.9 %all_to_all.39 = f32[8,32,4096]{2,1,0:T(8,128)S(1)} all-to-all(f32[8,32,4096]{2,1,0:T(8,128)S(1)} %bitcast.69), channel_id=1, replica_groups=mesh['vox'=32,'frm'=8] {'frm'}, dimensions={0} | all-to-all | bytes 8388608 | tf_op jit(solution)/shard_map/all_to_all | solution.py:28
  430.1 2.3 copy.10
  (6 shorter events, 0.1 us)
Async XLA Ops:
  7.2 317.3 %copy-start = (f32[256,64]{0,1:T(8,128)S(1)}, f32[256,64]{0,1:T(8,128)}, u32[]{:S(2)}) copy-start(f32[256,64]{0,1:T(8,128)} %param.6) | copy-start | bytes 196612
  7.2 317.3 %all-reduce.2.cloned.1.call-start = ((), (), s32[]{:S(2)}) async-start(), calls=%async_computation.2 | async-start | bytes 524288 | tf_op jit(solution)/shard_map/psum | solution.py:23
  64.1 2.0 copy-start.1
  366.2 5.4 %copy-start.2 = (f32[32,8,4096]{2,0,1:T(8,128)S(1)}, f32[32,8,4096]{2,0,1:T(8,128)}, u32[]{:S(2)}) copy-start(f32[32,8,4096]{2,0,1:T(8,128)} %copy-done.1) | copy-start | bytes 12582916
  366.5 8.7 %copy-start.3 = (f32[64,256]{1,0:T(8,128)}, f32[64,256]{1,0:T(8,128)S(1)}, u32[]{:S(2)}) copy-start(f32[64,256]{1,0:T(8,128)S(1)} %fusion) | copy-start | bytes 196612
Sparse Core Ops, SparseCore 0:
  70.5 253.9 all-reduce.1
where the time goes:
time: 440 us; the launch traced here: 439 us
  waiting for transfers between devices  254 us (58%)
  blocking collectives  109 us (25%)
  other arithmetic  36.2 us (8%)
  matrix products  18.3 us (4%)
  between operations  14.2 us (3%)
  local copies, waits for them, and re-layouts  7.04 us (2%)
    psum x1, waiting for transfers between devices, body(): gram = lax.psum(contract_cols(columns, columns), ('vox', 'frm'))  254 us
    all_to_all x1, blocking collectives, body(): lax.all_to_all(cleaned, 'frm', split_axis=0, concat_axis=1, tiled=True)  54.9 us
    all_to_all x1, blocking collectives, body(): lax.all_to_all(casorati, 'frm', split_axis=1, concat_axis=0, tiled=True)  54.4 us
    another operation x9, other arithmetic, orthonormal(): lower = jnp.linalg.cholesky(small)  19.6 us
    another operation x6, other arithmetic, orthonormal(): return jax.scipy.linalg.solve_triangular(lower, projected.T, lower=True).T  16.6 us
  transfers between devices with their start and end apart: 1, of which 1 were waited for; matrix products, arithmetic and copies ran while one was open for 0% of the time, Pallas kernels for 0%

commit v1 on v0

v1 whole, which is shorter than its diff:
```python
import functools

import jax
import jax.numpy as jnp
from jax import lax
from jax.experimental import pallas as pl
from jax.experimental.pallas import tpu as pltpu
from jax.sharding import Mesh
from jax.sharding import PartitionSpec as P

ITERS = 3
FRAMES = 256
VECS = 64
BLOCK = 64
SIZES = dict(x=4, z=8, y=4, core=2)
FRM = ("y", "core")
VOX = ("x", "z")
NT = (((1,), (1,)), ((), ()))
PAIRS = [(i, j) for i in range(FRAMES // BLOCK) for j in range(i, FRAMES // BLOCK)]


def split(value):
    high = value.astype(jnp.bfloat16)
    low = (value - high.astype(jnp.float32)).astype(jnp.bfloat16)
    return high, low


def gram_kernel(columns_ref, packed_ref, main, cross):
    chunk = 512
    main[...] = jnp.zeros_like(main)
    cross[...] = jnp.zeros_like(cross)

    @pl.loop(0, columns_ref.shape[1] // chunk)
    def _(step):
        high, low = split(columns_ref[:, pl.ds(pl.multiple_of(step * chunk, chunk), chunk)])
        main[...] += lax.dot_general(high, high, NT, preferred_element_type=jnp.float32)
        cross[...] += lax.dot_general(high, low, NT, preferred_element_type=jnp.float32)

    total = main[...] + cross[...] + cross[...].T
    packed_ref[...] = jnp.concatenate(
        [total[i * BLOCK : (i + 1) * BLOCK, j * BLOCK : (j + 1) * BLOCK] for i, j in PAIRS], axis=1
    )


def gram_packed(columns):
    return pl.pallas_call(
        gram_kernel,
        out_shape=jax.ShapeDtypeStruct((BLOCK, BLOCK * len(PAIRS)), jnp.float32),
        in_specs=[pl.BlockSpec(memory_space=pltpu.VMEM)],
        out_specs=pl.BlockSpec(memory_space=pltpu.VMEM),
        scratch_shapes=[pltpu.VMEM((FRAMES, FRAMES), jnp.float32)] * 2,
        cost_estimate=pl.CostEstimate(flops=2 * 3 * FRAMES * FRAMES * 4096, bytes_accessed=4 << 20, transcendentals=0),
        name="gram",
    )(columns)


def inverse_factor(small):
    size = small.shape[0]
    shape = (8, 2 * size)
    sublane = lax.broadcasted_iota(jnp.int32, shape, 0)
    wide = jnp.concatenate([small, jnp.eye(size, dtype=jnp.float32)], axis=1)
    rows = [wide[8 * i : 8 * i + 8, :] for i in range(size // 8)]

    def spread_row(value, row):
        return jnp.broadcast_to(value[row : row + 1, :], shape)

    scaled = []
    for block in range(size // 8):
        held = {
            i: [jnp.broadcast_to(rows[i][:, 8 * block + t : 8 * block + t + 1], shape) for t in range(8)]
            for i in range(block, size // 8)
        }
        diagonal, mine = held[block], rows[block]
        pivots = jnp.zeros(shape, jnp.float32)
        inverses, pivot_rows, heads = [], [], []
        for t in range(8):
            pivot = spread_row(diagonal[t], t)
            pivots = jnp.where(sublane == t, pivot, pivots)
            inverse = 1.0 / pivot
            factor = jnp.where(sublane > t, diagonal[t] * inverse, 0.0)
            row = spread_row(mine, t)
            mine = mine - factor * row
            head = {}
            for j in range(t + 1, 8):
                head[j] = spread_row(diagonal[j], t)
                diagonal[j] = diagonal[j] - factor * head[j]
            inverses.append(inverse)
            pivot_rows.append(row)
            heads.append(head)
        for i in range(block + 1, size // 8):
            for t in range(8):
                factor = held[i][t] * inverses[t]
                rows[i] = rows[i] - factor * pivot_rows[t]
                for j in range(t + 1, 8):
                    held[i][j] = held[i][j] - factor * heads[t][j]
        scaled.append(mine * lax.rsqrt(pivots))
    return jnp.concatenate(scaled, axis=0)[:, size:]


def iterate_kernel(packed_ref, start_ref, turned_ref, vectors_ref, gram):
    for n, (i, j) in enumerate(PAIRS):
        block = packed_ref[:, n * BLOCK : (n + 1) * BLOCK]
        gram[i * BLOCK : (i + 1) * BLOCK, j * BLOCK : (j + 1) * BLOCK] = block
        if i != j:
            gram[j * BLOCK : (j + 1) * BLOCK, i * BLOCK : (i + 1) * BLOCK] = block.T
    dot = functools.partial(
        lax.dot_general, precision=lax.Precision.HIGHEST, preferred_element_type=jnp.float32
    )
    turned_ref[...] = start_ref[...].T

    @pl.loop(0, ITERS)
    def _(step):
        projected = dot(turned_ref[...], gram[...], NT)
        small = dot(projected, projected, NT)
        turned_ref[...] = dot(inverse_factor(small), projected, (((1,), (0,)), ((), ())))

    vectors_ref[...] = turned_ref[...].T


def iterate(packed, start):
    return pl.pallas_call(
        iterate_kernel,
        out_shape=(
            jax.ShapeDtypeStruct((VECS, FRAMES), jnp.float32),
            jax.ShapeDtypeStruct((FRAMES, VECS), jnp.float32),
        ),
        in_specs=[pl.BlockSpec(memory_space=pltpu.VMEM)] * 2,
        out_specs=(pl.BlockSpec(memory_space=pltpu.VMEM),) * 2,
        scratch_shapes=[pltpu.VMEM((FRAMES, FRAMES), jnp.float32)],
        name="iterate",
    )(packed, start)


def exchange(value, axis, mask):
    pairs = [(2 * i + 1, 2 * (i ^ mask) + 1) for i in range(SIZES[axis])]
    return lax.ppermute(value, (axis, "core"), pairs)


def total_of(packed):
    y, core = lax.axis_index("y"), lax.axis_index("core")
    value = packed + lax.ppermute(packed, "core", [(0, 1)])
    stages = [(1, (y ^ (y >> 1)) & 1), (3, (y >> 1) & 1)]
    for mask, side in stages:
        half = value.shape[0] // 2
        low, high = value[:half], value[half:]
        kept, sent = jnp.where(side == 1, high, low), jnp.where(side == 1, low, high)
        value = kept + exchange(sent, "y", mask)
    for axis, mask in (("x", 1), ("x", 3), ("z", 1), ("z", 2), ("z", 6)):
        value = value + exchange(value, axis, mask)
    for mask, side in reversed(stages):
        other = exchange(value, "y", mask)
        value = jnp.where(side == 1, jnp.concatenate([other, value]), jnp.concatenate([value, other]))
    return jnp.where(core == 1, value, lax.ppermute(value, "core", [(1, 0)]))


def filter_kernel(where_ref, vectors_ref, *refs):
    casorati_ref, filtered_ref = refs[-2:]
    high, low = split(vectors_ref[...])
    left = jnp.concatenate([high, high, low], axis=1)
    for n, image_ref in enumerate(refs[:-2]):

        @pl.when(pl.program_id(0) == n)
        def _():
            top, bottom = split(image_ref[...])
            right = jnp.concatenate([top, bottom, top], axis=0)
            filtered_ref[...] = casorati_ref[...] - jnp.dot(left, right, preferred_element_type=jnp.float32)


def filtered_of(casorati, mine, pieces):
    rows = casorati.shape[0]
    width = pieces[0][1].shape[1]
    where = jnp.stack([w for w, _ in pieces]).astype(jnp.int32)
    block = pl.BlockSpec((rows, width), lambda n, where: (0, where[n]))
    return pl.pallas_call(
        filter_kernel,
        out_shape=jax.ShapeDtypeStruct(casorati.shape, jnp.float32),
        grid_spec=pltpu.PrefetchScalarGridSpec(
            num_scalar_prefetch=1,
            grid=(len(pieces),),
            in_specs=[pl.BlockSpec((rows, VECS), lambda n, where: (0, 0))]
            + [pl.BlockSpec((VECS, width), lambda n, where: (0, 0))] * len(pieces)
            + [block],
            out_specs=block,
        ),
        cost_estimate=pl.CostEstimate(flops=2 * 3 * VECS * rows * width * len(pieces), bytes_accessed=16 << 20, transcendentals=0),
        name="subtract",
    )(where, mine, *[image for _, image in pieces], casorati)


def shift(value, step):
    return lax.ppermute(value, "y", [(i, (i + step) % SIZES["y"]) for i in range(SIZES["y"])])


def swap(value):
    return lax.ppermute(value, "core", [(0, 1), (1, 0)])


def body(casorati, start):
    y, core = lax.axis_index("y"), lax.axis_index("core")
    columns = lax.all_to_all(casorati, FRM, split_axis=1, concat_axis=0, tiled=True)
    turned, vectors = iterate(total_of(gram_packed(columns)), start)
    image = lax.dot_general(
        turned, columns, (((1,), (0,)), ((), ())), precision=lax.Precision.HIGH, preferred_element_type=jnp.float32
    )
    half = image.shape[1] // 2
    left, right = image[:, :half], image[:, half:]
    up_left, down_right = shift(left, 1), shift(right, -1)
    up_right, down_left = shift(right, 1), shift(left, -1)
    far_left, far_right = shift(up_left, 1), shift(down_right, -1)
    parts = [(0, 0, left), (0, 1, right), (-1, 0, up_left), (1, 1, down_right)]
    parts += [(-1, 1, up_right), (1, 0, down_left), (2, 0, far_left), (2, 1, far_right)]
    pieces = []
    for step, side, value in parts:
        chip = (y + step) % SIZES["y"]
        pieces.append(((chip * 2 + core) * 2 + side, value))
        pieces.append(((chip * 2 + 1 - core) * 2 + side, swap(value)))
    mine = lax.dynamic_slice_in_dim(vectors, (y * 2 + core) * casorati.shape[0], casorati.shape[0], axis=0)
    return vectors, filtered_of(casorati, mine, pieces)


def solution(mesh):
    inner = Mesh(mesh.devices.reshape(4, 8, 4, 2), ("x", "z", "y", "core"))
    return jax.shard_map(
        body,
        mesh=inner,
        in_specs=(P(FRM, VOX), P()),
        out_specs=(P(), P(FRM, VOX)),
        check_vma=False,
    )
```

time: 440 us -> 198 us (0.45)
  waiting for transfers between devices: 254 us -> 47.6 us
  blocking collectives: 109 us -> 55.1 us
  starting transfers between devices: 0.04 us -> 50.7 us
  other arithmetic: 36.2 us -> 1.72 us
  Pallas kernels: 0 us -> 31.9 us
  matrix products: 18.3 us -> 3.67 us
  between operations: 14.2 us -> 0.91 us
    psum x1 -> x0, waiting for transfers between devices: 254 us -> none  [body(): gram = lax.psum(contract_cols(columns, columns), ('vox', 'frm'))]
    all_to_all x2 -> x1, blocking collectives: 109 us -> 55.1 us  [body(): lax.all_to_all(casorati, FRM, split_axis=1, concat_axis=0, tiled=True)]
    ppermute x0 -> x25, starting transfers between devices: none -> 50.7 us  [the longest x9 31 us: exchange(): return lax.ppermute(value, (axis, 'core'), pairs)]
    ppermute x0 -> x25, waiting for transfers between devices: none -> 47.6 us  [the longest x6 24.2 us: shift(): lax.ppermute(value, 'y', [(i, (i + step) % SIZES['y']) for i in range(SIZ...]
    another operation x15 -> x0, other arithmetic: 36.2 us -> none  [the longest x9 19.6 us: orthonormal(): lower = jnp.linalg.cholesky(small)]
    pallas_call x0 -> x3, Pallas kernels: none -> 31.9 us  [the longest x1 15.8 us: filtered_of(): pl.pallas_call(filter_kernel, out_shape=jax.ShapeDtypeStruct(casorati.sha...]
    dot_general x9 -> x1, matrix products: 17.5 us -> 3.67 us  [body(): lax.dot_general(turned, columns, (((1,), (0,)), ((), ())), precision=lax....]
  transfers between devices with their start and end apart: 1 -> 25, of which waited for: 1 -> 15; matrix products, arithmetic and copies ran while one was open for 0% -> 1% of each run, Pallas kernels for 0% -> 0%
where the time goes in v1:
time: 198 us; the launch traced here: 197 us
  blocking collectives  55.1 us (28%)
  starting transfers between devices  50.7 us (26%)
  waiting for transfers between devices  47.6 us (24%)
  Pallas kernels  31.9 us (16%)
  local copies, waits for them, and re-layouts  5.29 us (3%)
  matrix products  3.67 us (2%)
    all_to_all x1, blocking collectives, body(): lax.all_to_all(casorati, FRM, split_axis=1, concat_axis=0, tiled=True)  55.1 us
    ppermute x9, starting transfers between devices, exchange(): return lax.ppermute(value, (axis, 'core'), pairs)  31 us
    ppermute x6, waiting for transfers between devices, shift(): lax.ppermute(value, 'y', [(i, (i + step) % SIZES['y']) for i in range(SIZ...  24.2 us
    ppermute x9, waiting for transfers between devices, exchange(): return lax.ppermute(value, (axis, 'core'), pairs)  20.9 us
    pallas_call x1, Pallas kernels, filtered_of(): pl.pallas_call(filter_kernel, out_shape=jax.ShapeDtypeStruct(casorati.sha...  15.8 us
    pallas_call x1, Pallas kernels, iterate(): pl.pallas_call(iterate_kernel, out_shape=(jax.ShapeDtypeStruct((VECS, FRA...  10.3 us
    ppermute x8, starting transfers between devices, swap(): return lax.ppermute(value, 'core', [(0, 1), (1, 0)])  8.78 us
    ppermute x6, starting transfers between devices, shift(): lax.ppermute(value, 'y', [(i, (i + step) % SIZES['y']) for i in range(SIZ...  8.28 us
  transfers between devices with their start and end apart: 25, of which 15 were waited for; matrix products, arithmetic and copies ran while one was open for 1% of the time, Pallas kernels for 0%

profile of v1, /device:TPU:1, one launch (start us, length us, event | category | flops | bytes accessed | tf_op | source)
XLA Modules:
  0.0 196.9 jit_solution(8125349252015599475)
XLA Ops:
  0.6 2.5 %copy.9 = f32[4,8,8,4096]{3,2,0,1:T(8,128)S(1)} copy(f32[4,8,8,4096]{3,2,1,0:T(8,128)} %bitcast.28) | data formatting | bytes 8388608 | tf_op jit(solution)/shard_map/all_to_all | solution.py:200
  3.1 55.1 %all_to_all.19 = f32[32,8,4096]{2,0,1:T(8,128)} all-to-all(f32[32,8,4096]{2,0,1:T(8,128)S(1)} %bitcast.27), channel_id=1, replica_groups=mesh['x'=4,'z'=8,'y'=4,'core'=2] {'y','core'}, dimensions={1} | all-to-all | bytes 8388608 | tf_op jit(solution)/shard_map/all_to_all | solution.py:200
  58.2 5.9 %gram.1 = f32[64,640]{1,0:T(8,128)} custom-call(f32[256,4096]{1,0:T(8,128)} %bitcast.25), custom_call_target="tpu_custom_call" | custom-call | flops 1610612736 | bytes 4194304 | tf_op jit(solution)/shard_map/gram/pallas_call | solution.py:46
  64.1 1.3 collective-permute-start
  65.4 2.2 %collective-permute-done = f32[64,640]{1,0:T(8,128)S(1)} collective-permute-done((f32[64,640]{1,0:T(8,128)}, f32[64,640]{1,0:T(8,128)S(1)}, u32[]{:S(2)}, u32[]{:S(2)}) %collective-permute-start) | collective-permute-done | bytes 163872 | tf_op jit(solution)/shard_map/ppermute | solution.py:141
  67.6 0.9 add.115
  68.5 2.7 %collective-permute-start.1 = (f32[32,640]{1,0:T(8,128)S(1)}, f32[32,640]{1,0:T(8,128)S(1)}, u32[]{:S(2)}, u32[]{:S(2)}) collective-permute-start(f32[32,640]{1,0:T(8,128)S(1)} %slice_select_fusion), channel_id=1, source_target_pairs={{1,3},{3,1},{5,7},{7,5},{9,11},{11,9},{13,15},{15,13},{17,19},{19,... | collective-permute-start | bytes 245768 | tf_op jit(solution)/shard_map/ppermute | solution.py:136
  71.3 2.4 %collective-permute-done.1 = f32[32,640]{1,0:T(8,128)S(1)} collective-permute-done((f32[32,640]{1,0:T(8,128)S(1)}, f32[32,640]{1,0:T(8,128)S(1)}, u32[]{:S(2)}, u32[]{:S(2)}) %collective-permute-start.1) | collective-permute-done | bytes 81952 | tf_op jit(solution)/shard_map/ppermute | solution.py:136
  73.8 2.8 %collective-permute-start.2 = (f32[16,640]{1,0:T(8,128)S(1)}, f32[16,640]{1,0:T(8,128)S(1)}, u32[]{:S(2)}, u32[]{:S(2)}) collective-permute-start(f32[16,640]{1,0:T(8,128)S(1)} %slice_select_fusion.1), channel_id=1, source_target_pairs={{1,7},{3,5},{5,3},{7,1},{9,15},{11,13},{13,11},{15,9},{17,23},{19,... | collective-permute-start | bytes 122888 | tf_op jit(solution)/shard_map/ppermute | solution.py:136
  76.6 3.2 %collective-permute-done.2 = f32[16,640]{1,0:T(8,128)S(1)} collective-permute-done((f32[16,640]{1,0:T(8,128)S(1)}, f32[16,640]{1,0:T(8,128)S(1)}, u32[]{:S(2)}, u32[]{:S(2)}) %collective-permute-start.2) | collective-permute-done | bytes 40992 | tf_op jit(solution)/shard_map/ppermute | solution.py:136
  79.7 2.5 %collective-permute-start.3 = (f32[16,640]{1,0:T(8,128)S(1)}, f32[16,640]{1,0:T(8,128)S(1)}, u32[]{:S(2)}, u32[]{:S(2)}) collective-permute-start(f32[16,640]{1,0:T(8,128)S(1)} %select_add_fusion.1), channel_id=1, source_target_pairs={{1,65},{65,1},{129,193},{193,129},{3,67},{67,3},{131,195},{195,131... | collective-permute-start | bytes 122888 | tf_op jit(solution)/shard_map/ppermute | solution.py:136
  82.3 2.2 %collective-permute-done.3 = f32[16,640]{1,0:T(8,128)S(1)} collective-permute-done((f32[16,640]{1,0:T(8,128)S(1)}, f32[16,640]{1,0:T(8,128)S(1)}, u32[]{:S(2)}, u32[]{:S(2)}) %collective-permute-start.3) | collective-permute-done | bytes 40992 | tf_op jit(solution)/shard_map/ppermute | solution.py:136
  84.5 3.8 %collective-permute-start.4 = (f32[16,640]{1,0:T(8,128)S(1)}, f32[16,640]{1,0:T(8,128)S(1)}, u32[]{:S(2)}, u32[]{:S(2)}) collective-permute-start(f32[16,640]{1,0:T(8,128)S(1)} %add.118), channel_id=1, source_target_pairs={{1,193},{65,129},{129,65},{193,1},{3,195},{67,131},{131,67},{195,3... | collective-permute-start | bytes 122888 | tf_op jit(solution)/shard_map/ppermute | solution.py:136
  88.3 2.2 %collective-permute-done.4 = f32[16,640]{1,0:T(8,128)S(1)} collective-permute-done((f32[16,640]{1,0:T(8,128)S(1)}, f32[16,640]{1,0:T(8,128)S(1)}, u32[]{:S(2)}, u32[]{:S(2)}) %collective-permute-start.4) | collective-permute-done | bytes 40992 | tf_op jit(solution)/shard_map/ppermute | solution.py:136
  90.4 2.9 %collective-permute-start.5 = (f32[16,640]{1,0:T(8,128)S(1)}, f32[16,640]{1,0:T(8,128)S(1)}, u32[]{:S(2)}, u32[]{:S(2)}) collective-permute-start(f32[16,640]{1,0:T(8,128)S(1)} %add.119), channel_id=1, source_target_pairs={{1,9},{9,1},{17,25},{25,17},{33,41},{41,33},{49,57},{57,49},{3,11}... | collective-permute-start | bytes 122888 | tf_op jit(solution)/shard_map/ppermute | solution.py:136
  93.4 1.8 collective-permute-done.5
  95.2 4.5 %collective-permute-start.6 = (f32[16,640]{1,0:T(8,128)S(1)}, f32[16,640]{1,0:T(8,128)S(1)}, u32[]{:S(2)}, u32[]{:S(2)}) collective-permute-start(f32[16,640]{1,0:T(8,128)S(1)} %add.120), channel_id=1, source_target_pairs={{1,17},{9,25},{17,1},{25,9},{33,49},{41,57},{49,33},{57,41},{3,19}... | collective-permute-start | bytes 122888 | tf_op jit(solution)/shard_map/ppermute | solution.py:136
  99.7 1.4 collective-permute-done.6
  101.1 7.1 %collective-permute-start.7 = (f32[16,640]{1,0:T(8,128)S(1)}, f32[16,640]{1,0:T(8,128)S(1)}, u32[]{:S(2)}, u32[]{:S(2)}) collective-permute-start(f32[16,640]{1,0:T(8,128)S(1)} %add.121), channel_id=1, source_target_pairs={{1,49},{9,57},{17,33},{25,41},{33,17},{41,25},{49,1},{57,9},{3,51}... | collective-permute-start | bytes 122888 | tf_op jit(solution)/shard_map/ppermute | solution.py:136
  108.2 1.4 collective-permute-done.7
  109.5 2.8 %collective-permute-start.8 = (f32[16,640]{1,0:T(8,128)S(1)}, f32[16,640]{1,0:T(8,128)S(1)}, u32[]{:S(2)}, u32[]{:S(2)}) collective-permute-start(f32[16,640]{1,0:T(8,128)S(1)} %add.122), channel_id=1, source_target_pairs={{1,7},{3,5},{5,3},{7,1},{9,15},{11,13},{13,11},{15,9},{17,23},{19,... | collective-permute-start | bytes 122888 | tf_op jit(solution)/shard_map/ppermute | solution.py:136
  112.3 3.2 %collective-permute-done.8 = f32[16,640]{1,0:T(8,128)S(1)} collective-permute-done((f32[16,640]{1,0:T(8,128)S(1)}, f32[16,640]{1,0:T(8,128)S(1)}, u32[]{:S(2)}, u32[]{:S(2)}) %collective-permute-start.8) | collective-permute-done | bytes 40992 | tf_op jit(solution)/shard_map/ppermute | solution.py:136
  115.5 1.9 collective-permute-start.9
  117.4 3.3 %collective-permute-done.9 = f32[32,640]{1,0:T(8,128)S(1)} collective-permute-done((f32[32,640]{1,0:T(8,128)S(1)}, f32[32,640]{1,0:T(8,128)S(1)}, u32[]{:S(2)}, u32[]{:S(2)}) %collective-permute-start.9) | collective-permute-done | bytes 81952 | tf_op jit(solution)/shard_map/ppermute | solution.py:136
  120.7 1.3 collective-permute-start.10
  122.0 0.7 copy.5.start_ref
  122.8 0.2 collective-permute-done.10
  123.0 0.7 broadcast_select_fusion.packed_ref
  123.7 10.3 %iterate.1 = (f32[64,256]{1,0:T(8,128)}, f32[256,64]{1,0:T(8,128)}) custom-call(f32[64,640]{1,0:T(8,128)} %broadcast_select_fusion.packed_ref, f32[256,64]{1,0:T(8,128)} %copy.5.start_ref), custom_call_target="tpu_custom_call" | custom-call | tf_op jit(solution)/shard_map/iterate/pallas_call | solution.py:121
  134.0 3.7 %fusion.1 = f32[64,4096]{1,0:T(8,128)S(1)} fusion(f32[64,256]{1,0:T(8,128)} %get-tuple-element.5, f32[256,4096]{1,0:T(8,128)} %bitcast.26), kind=kOutput, calls=%fused_computation.10 | convolution fusion | flops 402653184 | bytes 5308416 | tf_op jit(solution)/shard_map/dot_general | solution.py:202
  137.9 2.7 %collective-permute-start.15 = (f32[64,2048]{1,0:T(8,128)S(1)}, f32[64,2048]{1,0:T(8,128)S(1)}, u32[]{:S(2)}, u32[]{:S(2)}) collective-permute-start(f32[64,2048]{1,0:T(8,128)S(1)} %get-tuple-element.8.refs_2_), channel_id=1, source_target_pairs={{0,6},{2,0},{4,2},{6,4},{1,7},{3,1},{5,3},{7,5},{8,14},{10,8},{12,... | collective-permute-start | bytes 1572872 | tf_op jit(solution)/shard_map/ppermute | solution.py:191
  140.5 0.9 collective-permute-start.12
  141.5 2.7 %collective-permute-start.19 = (f32[64,2048]{1,0:T(8,128)S(1)}, f32[64,2048]{1,0:T(8,128)}, u32[]{:S(2)}, u32[]{:S(2)}) collective-permute-start(f32[64,2048]{1,0:T(8,128)S(1)} %get-tuple-element.9.refs_0_), channel_id=1, source_target_pairs={{0,6},{2,0},{4,2},{6,4},{1,7},{3,1},{5,3},{7,5},{8,14},{10,8},{12,... | collective-permute-start | bytes 1572872 | tf_op jit(solution)/shard_map/ppermute | solution.py:191
  144.1 8.0 %collective-permute-done.17.refs_8_ = f32[64,2048]{1,0:T(8,128)S(1)} collective-permute-done((f32[64,2048]{1,0:T(8,128)S(1)}, f32[64,2048]{1,0:T(8,128)S(1)}, u32[]{:S(2)}, u32[]{:S(2)}) %collective-permute-start.17) | collective-permute-done | bytes 524320 | tf_op jit(solution)/shard_map/ppermute | solution.py:191
  152.2 2.1 %collective-permute-start.11 = (f32[64,2048]{1,0:T(8,128)S(1)}, f32[64,2048]{1,0:T(8,128)S(1)}, u32[]{:S(2)}, u32[]{:S(2)}) collective-permute-start(f32[64,2048]{1,0:T(8,128)S(1)} %get-tuple-element.9.refs_0_), channel_id=1, source_target_pairs={{0,1},{1,0},{2,3},{3,2},{4,5},{5,4},{6,7},{7,6},{8,9},{9,8},{10,11... | collective-permute-start | bytes 1572872 | tf_op jit(solution)/shard_map/ppermute | solution.py:195
  154.3 2.9 %collective-permute-start.23 = (f32[64,2048]{1,0:T(8,128)S(1)}, f32[64,2048]{1,0:T(8,128)}, u32[]{:S(2)}, u32[]{:S(2)}) collective-permute-start(f32[64,2048]{1,0:T(8,128)S(1)} %collective-permute-done.15.refs_6_), channel_id=1, source_target_pairs={{0,6},{2,0},{4,2},{6,4},{1,7},{3,1},{5,3},{7,5},{8,14},{10,8},{12,... | collective-permute-start | bytes 1572872 | tf_op jit(solution)/shard_map/ppermute | solution.py:191
  157.2 6.2 %collective-permute-done.13.refs_4_ = f32[64,2048]{1,0:T(8,128)S(1)} collective-permute-done((f32[64,2048]{1,0:T(8,128)S(1)}, f32[64,2048]{1,0:T(8,128)S(1)}, u32[]{:S(2)}, u32[]{:S(2)}) %collective-permute-start.13) | collective-permute-done | bytes 524320 | tf_op jit(solution)/shard_map/ppermute | solution.py:191
  163.4 1.6 collective-permute-start.16
  165.0 0.3 collective-permute-start.14
  165.3 0.2 collective-permute-start.20
  165.5 8.1 %collective-permute-done.23.refs_14_ = f32[64,2048]{1,0:T(8,128)} collective-permute-done((f32[64,2048]{1,0:T(8,128)S(1)}, f32[64,2048]{1,0:T(8,128)}, u32[]{:S(2)}, u32[]{:S(2)}) %collective-permute-start.23) | collective-permute-done | bytes 524320 | tf_op jit(solution)/shard_map/ppermute | solution.py:191
  173.6 1.5 collective-permute-start.24
  175.1 1.8 collective-permute-done.21.refs_12_
  177.0 2.1 %collective-permute-start.22 = (f32[64,2048]{1,0:T(8,128)}, f32[64,2048]{1,0:T(8,128)}, u32[]{:S(2)}, u32[]{:S(2)}) collective-permute-start(f32[64,2048]{1,0:T(8,128)} %collective-permute-done.21.refs_12_), channel_id=1, source_target_pairs={{0,1},{1,0},{2,3},{3,2},{4,5},{5,4},{6,7},{7,6},{8,9},{9,8},{10,11... | collective-permute-start | bytes 1572872 | tf_op jit(solution)/shard_map/ppermute | solution.py:195
  179.1 0.6 stack.67.where_ref
  179.7 0.7 copy.6
  180.4 0.6 constant_dynamic-slice_fusion.vectors_ref
  181.1 15.8 %subtract.1 = f32[32,32768]{1,0:T(8,128)} custom-call(s32[16]{0:T(128)} %stack.67.where_ref, f32[32,64]{1,0:T(8,128)} %constant_dynamic-slice_fusion.vectors_ref, f32[64,2048]{1,0:T(8,128)} %copy-done.1, f32[64,2048]{1,0:T(8,128)} %copy-done.6, f32[64,2048]{1,0:T(8,128)} %copy-done, f32[64,2048]{1,0:T(8,128)} %copy-done.4, f32[64,2048]{1,0:T(8,128)} %copy-done.5, ...), custom_call_target="tpu_custom_call" | custom-call | flops 402653184 | bytes 16777216 | tf_op jit(solution)/shard_map/subtract/pallas_call | solution.py:174
  (46 shorter events, 0.5 us)
Async XLA Ops:
  58.2 63.8 %copy-start.9 = (f32[256,64]{0,1:T(8,128)S(1)}, f32[256,64]{0,1:T(8,128)}, u32[]{:S(2)}) copy-start(f32[256,64]{0,1:T(8,128)} %param.3) | copy-start | bytes 196612
  64.1 3.5 %collective-permute-start = (f32[64,640]{1,0:T(8,128)}, f32[64,640]{1,0:T(8,128)S(1)}, u32[]{:S(2)}, u32[]{:S(2)}) collective-permute-start(f32[64,640]{1,0:T(8,128)} %gram.1), channel_id=1, source_target_pairs={{0,1},{2,3},{4,5},{6,7},{8,9},{10,11},{12,13},{14,15},{16,17},{18,... | collective-permute-start | bytes 491528 | tf_op jit(solution)/shard_map/ppermute | solution.py:141
  68.5 5.2 %collective-permute-start.1 = (f32[32,640]{1,0:T(8,128)S(1)}, f32[32,640]{1,0:T(8,128)S(1)}, u32[]{:S(2)}, u32[]{:S(2)}) collective-permute-start(f32[32,640]{1,0:T(8,128)S(1)} %slice_select_fusion), channel_id=1, source_target_pairs={{1,3},{3,1},{5,7},{7,5},{9,11},{11,9},{13,15},{15,13},{17,19},{19,... | collective-permute-start | bytes 245768 | tf_op jit(solution)/shard_map/ppermute | solution.py:136
  73.8 6.0 %collective-permute-start.2 = (f32[16,640]{1,0:T(8,128)S(1)}, f32[16,640]{1,0:T(8,128)S(1)}, u32[]{:S(2)}, u32[]{:S(2)}) collective-permute-start(f32[16,640]{1,0:T(8,128)S(1)} %slice_select_fusion.1), channel_id=1, source_target_pairs={{1,7},{3,5},{5,3},{7,1},{9,15},{11,13},{13,11},{15,9},{17,23},{19,... | collective-permute-start | bytes 122888 | tf_op jit(solution)/shard_map/ppermute | solution.py:136
  79.7 4.7 %collective-permute-start.3 = (f32[16,640]{1,0:T(8,128)S(1)}, f32[16,640]{1,0:T(8,128)S(1)}, u32[]{:S(2)}, u32[]{:S(2)}) collective-permute-start(f32[16,640]{1,0:T(8,128)S(1)} %select_add_fusion.1), channel_id=1, source_target_pairs={{1,65},{65,1},{129,193},{193,129},{3,67},{67,3},{131,195},{195,131... | collective-permute-start | bytes 122888 | tf_op jit(solution)/shard_map/ppermute | solution.py:136
  84.5 5.9 %collective-permute-start.4 = (f32[16,640]{1,0:T(8,128)S(1)}, f32[16,640]{1,0:T(8,128)S(1)}, u32[]{:S(2)}, u32[]{:S(2)}) collective-permute-start(f32[16,640]{1,0:T(8,128)S(1)} %add.118), channel_id=1, source_target_pairs={{1,193},{65,129},{129,65},{193,1},{3,195},{67,131},{131,67},{195,3... | collective-permute-start | bytes 122888 | tf_op jit(solution)/shard_map/ppermute | solution.py:136
  90.4 4.7 %collective-permute-start.5 = (f32[16,640]{1,0:T(8,128)S(1)}, f32[16,640]{1,0:T(8,128)S(1)}, u32[]{:S(2)}, u32[]{:S(2)}) collective-permute-start(f32[16,640]{1,0:T(8,128)S(1)} %add.119), channel_id=1, source_target_pairs={{1,9},{9,1},{17,25},{25,17},{33,41},{41,33},{49,57},{57,49},{3,11}... | collective-permute-start | bytes 122888 | tf_op jit(solution)/shard_map/ppermute | solution.py:136
  95.2 5.9 %collective-permute-start.6 = (f32[16,640]{1,0:T(8,128)S(1)}, f32[16,640]{1,0:T(8,128)S(1)}, u32[]{:S(2)}, u32[]{:S(2)}) collective-permute-start(f32[16,640]{1,0:T(8,128)S(1)} %add.120), channel_id=1, source_target_pairs={{1,17},{9,25},{17,1},{25,9},{33,49},{41,57},{49,33},{57,41},{3,19}... | collective-permute-start | bytes 122888 | tf_op jit(solution)/shard_map/ppermute | solution.py:136
  101.1 8.5 %collective-permute-start.7 = (f32[16,640]{1,0:T(8,128)S(1)}, f32[16,640]{1,0:T(8,128)S(1)}, u32[]{:S(2)}, u32[]{:S(2)}) collective-permute-start(f32[16,640]{1,0:T(8,128)S(1)} %add.121), channel_id=1, source_target_pairs={{1,49},{9,57},{17,33},{25,41},{33,17},{41,25},{49,1},{57,9},{3,51}... | collective-permute-start | bytes 122888 | tf_op jit(solution)/shard_map/ppermute | solution.py:136
  109.5 5.9 %collective-permute-start.8 = (f32[16,640]{1,0:T(8,128)S(1)}, f32[16,640]{1,0:T(8,128)S(1)}, u32[]{:S(2)}, u32[]{:S(2)}) collective-permute-start(f32[16,640]{1,0:T(8,128)S(1)} %add.122), channel_id=1, source_target_pairs={{1,7},{3,5},{5,3},{7,1},{9,15},{11,13},{13,11},{15,9},{17,23},{19,... | collective-permute-start | bytes 122888 | tf_op jit(solution)/shard_map/ppermute | solution.py:136
  115.5 5.2 %collective-permute-start.9 = (f32[32,640]{1,0:T(8,128)S(1)}, f32[32,640]{1,0:T(8,128)S(1)}, u32[]{:S(2)}, u32[]{:S(2)}) collective-permute-start(f32[32,640]{1,0:T(8,128)S(1)} %maximum_select_fusion.1), channel_id=1, source_target_pairs={{1,3},{3,1},{5,7},{7,5},{9,11},{11,9},{13,15},{15,13},{17,19},{19,... | collective-permute-start | bytes 245768 | tf_op jit(solution)/shard_map/ppermute | solution.py:136
  120.7 2.3 %collective-permute-start.10 = (f32[64,640]{1,0:T(8,128)S(1)}, f32[64,640]{1,0:T(8,128)S(1)}, u32[]{:S(2)}, u32[]{:S(2)}) collective-permute-start(f32[64,640]{1,0:T(8,128)S(1)} %maximum_select_fusion), channel_id=1, source_target_pairs={{1,0},{3,2},{5,4},{7,6},{9,8},{11,10},{13,12},{15,14},{17,16},{19,... | collective-permute-start | bytes 491528 | tf_op jit(solution)/shard_map/ppermute | solution.py:153
  134.0 45.7 %copy-start.8 = (f32[256,64]{1,0:T(8,128)S(1)}, f32[256,64]{1,0:T(8,128)}, u32[]{:S(2)}) copy-start(f32[256,64]{1,0:T(8,128)} %get-tuple-element.6) | copy-start | bytes 196612
  137.7 43.3 %copy-start = (f32[64,2048]{1,0:T(8,128)}, f32[64,2048]{1,0:T(8,128)S(1)}, u32[]{:S(2)}) copy-start(f32[64,2048]{1,0:T(8,128)S(1)} %get-tuple-element.8.refs_2_) | copy-start | bytes 1572868
  137.8 43.3 %copy-start.1 = (f32[64,2048]{1,0:T(8,128)}, f32[64,2048]{1,0:T(8,128)S(1)}, u32[]{:S(2)}) copy-start(f32[64,2048]{1,0:T(8,128)S(1)} %get-tuple-element.9.refs_0_) | copy-start | bytes 1572868
  137.8 14.4 %collective-permute-start.17 = (f32[64,2048]{1,0:T(8,128)S(1)}, f32[64,2048]{1,0:T(8,128)S(1)}, u32[]{:S(2)}, u32[]{:S(2)}) collective-permute-start(f32[64,2048]{1,0:T(8,128)S(1)} %get-tuple-element.8.refs_2_), channel_id=1, source_target_pairs={{0,2},{2,4},{4,6},{6,0},{1,3},{3,5},{5,7},{7,1},{8,10},{10,12},{12... | collective-permute-start | bytes 1572872 | tf_op jit(solution)/shard_map/ppermute | solution.py:191
  137.9 16.4 %collective-permute-start.15 = (f32[64,2048]{1,0:T(8,128)S(1)}, f32[64,2048]{1,0:T(8,128)S(1)}, u32[]{:S(2)}, u32[]{:S(2)}) collective-permute-start(f32[64,2048]{1,0:T(8,128)S(1)} %get-tuple-element.8.refs_2_), channel_id=1, source_target_pairs={{0,6},{2,0},{4,2},{6,4},{1,7},{3,1},{5,3},{7,5},{8,14},{10,8},{12,... | collective-permute-start | bytes 1572872 | tf_op jit(solution)/shard_map/ppermute | solution.py:191
  140.5 13.8 %collective-permute-start.12 = (f32[64,2048]{1,0:T(8,128)S(1)}, f32[64,2048]{1,0:T(8,128)S(1)}, u32[]{:S(2)}, u32[]{:S(2)}) collective-permute-start(f32[64,2048]{1,0:T(8,128)S(1)} %get-tuple-element.8.refs_2_), channel_id=1, source_target_pairs={{0,1},{1,0},{2,3},{3,2},{4,5},{5,4},{6,7},{7,6},{8,9},{9,8},{10,11... | collective-permute-start | bytes 1572872 | tf_op jit(solution)/shard_map/ppermute | solution.py:195
  141.5 21.9 %collective-permute-start.13 = (f32[64,2048]{1,0:T(8,128)S(1)}, f32[64,2048]{1,0:T(8,128)S(1)}, u32[]{:S(2)}, u32[]{:S(2)}) collective-permute-start(f32[64,2048]{1,0:T(8,128)S(1)} %get-tuple-element.9.refs_0_), channel_id=1, source_target_pairs={{0,2},{2,4},{4,6},{6,0},{1,3},{3,5},{5,7},{7,1},{8,10},{10,12},{12... | collective-permute-start | bytes 1572872 | tf_op jit(solution)/shard_map/ppermute | solution.py:191
  141.5 22.0 %collective-permute-start.19 = (f32[64,2048]{1,0:T(8,128)S(1)}, f32[64,2048]{1,0:T(8,128)}, u32[]{:S(2)}, u32[]{:S(2)}) collective-permute-start(f32[64,2048]{1,0:T(8,128)S(1)} %get-tuple-element.9.refs_0_), channel_id=1, source_target_pairs={{0,6},{2,0},{4,2},{6,4},{1,7},{3,1},{5,3},{7,5},{8,14},{10,8},{12,... | collective-permute-start | bytes 1572872 | tf_op jit(solution)/shard_map/ppermute | solution.py:191
  152.2 28.9 %copy-start.2 = (f32[64,2048]{1,0:T(8,128)}, f32[64,2048]{1,0:T(8,128)S(1)}, u32[]{:S(2)}) copy-start(f32[64,2048]{1,0:T(8,128)S(1)} %collective-permute-done.17.refs_8_) | copy-start | bytes 1572868
  152.2 12.8 %collective-permute-start.11 = (f32[64,2048]{1,0:T(8,128)S(1)}, f32[64,2048]{1,0:T(8,128)S(1)}, u32[]{:S(2)}, u32[]{:S(2)}) collective-permute-start(f32[64,2048]{1,0:T(8,128)S(1)} %get-tuple-element.9.refs_0_), channel_id=1, source_target_pairs={{0,1},{1,0},{2,3},{3,2},{4,5},{5,4},{6,7},{7,6},{8,9},{9,8},{10,11... | collective-permute-start | bytes 1572872 | tf_op jit(solution)/shard_map/ppermute | solution.py:195
  154.2 26.9 %copy-start.3 = (f32[64,2048]{1,0:T(8,128)}, f32[64,2048]{1,0:T(8,128)S(1)}, u32[]{:S(2)}) copy-start(f32[64,2048]{1,0:T(8,128)S(1)} %collective-permute-done.15.refs_6_) | copy-start | bytes 1572868
  154.2 11.0 %collective-permute-start.18 = (f32[64,2048]{1,0:T(8,128)S(1)}, f32[64,2048]{1,0:T(8,128)S(1)}, u32[]{:S(2)}, u32[]{:S(2)}) collective-permute-start(f32[64,2048]{1,0:T(8,128)S(1)} %collective-permute-done.17.refs_8_), channel_id=1, source_target_pairs={{0,1},{1,0},{2,3},{3,2},{4,5},{5,4},{6,7},{7,6},{8,9},{9,8},{10,11... | collective-permute-start | bytes 1572872 | tf_op jit(solution)/shard_map/ppermute | solution.py:195
  154.3 26.8 %copy-start.4 = (f32[64,2048]{1,0:T(8,128)}, f32[64,2048]{1,0:T(8,128)S(1)}, u32[]{:S(2)}) copy-start(f32[64,2048]{1,0:T(8,128)S(1)} %collective-permute-done.12.refs_3_) | copy-start | bytes 1572868
  154.3 19.3 %collective-permute-start.23 = (f32[64,2048]{1,0:T(8,128)S(1)}, f32[64,2048]{1,0:T(8,128)}, u32[]{:S(2)}, u32[]{:S(2)}) collective-permute-start(f32[64,2048]{1,0:T(8,128)S(1)} %collective-permute-done.15.refs_6_), channel_id=1, source_target_pairs={{0,6},{2,0},{4,2},{6,4},{1,7},{3,1},{5,3},{7,5},{8,14},{10,8},{12,... | collective-permute-start | bytes 1572872 | tf_op jit(solution)/shard_map/ppermute | solution.py:191
  163.4 17.7 %copy-start.5 = (f32[64,2048]{1,0:T(8,128)}, f32[64,2048]{1,0:T(8,128)S(1)}, u32[]{:S(2)}) copy-start(f32[64,2048]{1,0:T(8,128)S(1)} %collective-permute-done.13.refs_4_) | copy-start | bytes 1572868
  163.4 13.6 %collective-permute-start.21 = (f32[64,2048]{1,0:T(8,128)S(1)}, f32[64,2048]{1,0:T(8,128)}, u32[]{:S(2)}, u32[]{:S(2)}) collective-permute-start(f32[64,2048]{1,0:T(8,128)S(1)} %collective-permute-done.13.refs_4_), channel_id=1, source_target_pairs={{0,2},{2,4},{4,6},{6,0},{1,3},{3,5},{5,7},{7,1},{8,10},{10,12},{12... | collective-permute-start | bytes 1572872 | tf_op jit(solution)/shard_map/ppermute | solution.py:191
  163.4 17.6 %collective-permute-start.16 = (f32[64,2048]{1,0:T(8,128)S(1)}, f32[64,2048]{1,0:T(8,128)}, u32[]{:S(2)}, u32[]{:S(2)}) collective-permute-start(f32[64,2048]{1,0:T(8,128)S(1)} %collective-permute-done.15.refs_6_), channel_id=1, source_target_pairs={{0,1},{1,0},{2,3},{3,2},{4,5},{5,4},{6,7},{7,6},{8,9},{9,8},{10,11... | collective-permute-start | bytes 1572872 | tf_op jit(solution)/shard_map/ppermute | solution.py:195
  165.0 12.0 %copy-start.6 = (f32[64,2048]{1,0:T(8,128)}, f32[64,2048]{1,0:T(8,128)S(1)}, u32[]{:S(2)}) copy-start(f32[64,2048]{1,0:T(8,128)S(1)} %collective-permute-done.11.refs_1_) | copy-start | bytes 1572868
  165.0 16.0 %collective-permute-start.14 = (f32[64,2048]{1,0:T(8,128)S(1)}, f32[64,2048]{1,0:T(8,128)}, u32[]{:S(2)}, u32[]{:S(2)}) collective-permute-start(f32[64,2048]{1,0:T(8,128)S(1)} %collective-permute-done.13.refs_4_), channel_id=1, source_target_pairs={{0,1},{1,0},{2,3},{3,2},{4,5},{5,4},{6,7},{7,6},{8,9},{9,8},{10,11... | collective-permute-start | bytes 1572872 | tf_op jit(solution)/shard_map/ppermute | solution.py:195
  165.3 11.7 %copy-start.7 = (f32[64,2048]{1,0:T(8,128)}, f32[64,2048]{1,0:T(8,128)S(1)}, u32[]{:S(2)}) copy-start(f32[64,2048]{1,0:T(8,128)S(1)} %collective-permute-done.18.refs_9_) | copy-start | bytes 1572868
  165.3 15.8 %collective-permute-start.20 = (f32[64,2048]{1,0:T(8,128)}, f32[64,2048]{1,0:T(8,128)}, u32[]{:S(2)}, u32[]{:S(2)}) collective-permute-start(f32[64,2048]{1,0:T(8,128)} %collective-permute-done.19.refs_10_), channel_id=1, source_target_pairs={{0,1},{1,0},{2,3},{3,2},{4,5},{5,4},{6,7},{7,6},{8,9},{9,8},{10,11... | collective-permute-start | bytes 1572872 | tf_op jit(solution)/shard_map/ppermute | solution.py:195
  173.6 7.4 %collective-permute-start.24 = (f32[64,2048]{1,0:T(8,128)}, f32[64,2048]{1,0:T(8,128)}, u32[]{:S(2)}, u32[]{:S(2)}) collective-permute-start(f32[64,2048]{1,0:T(8,128)} %collective-permute-done.23.refs_14_), channel_id=1, source_target_pairs={{0,1},{1,0},{2,3},{3,2},{4,5},{5,4},{6,7},{7,6},{8,9},{9,8},{10,11... | collective-permute-start | bytes 1572872 | tf_op jit(solution)/shard_map/ppermute | solution.py:195
  177.0 4.1 %collective-permute-start.22 = (f32[64,2048]{1,0:T(8,128)}, f32[64,2048]{1,0:T(8,128)}, u32[]{:S(2)}, u32[]{:S(2)}) collective-permute-start(f32[64,2048]{1,0:T(8,128)} %collective-permute-done.21.refs_12_), channel_id=1, source_target_pairs={{0,1},{1,0},{2,3},{3,2},{4,5},{5,4},{6,7},{7,6},{8,9},{9,8},{10,11... | collective-permute-start | bytes 1572872 | tf_op jit(solution)/shard_map/ppermute | solution.py:195

commit v2 on v1

v2 whole, which is shorter than its diff:
```python
import functools

import jax
import jax.numpy as jnp
from jax import lax
from jax.experimental import pallas as pl
from jax.experimental.pallas import tpu as pltpu
from jax.sharding import Mesh
from jax.sharding import PartitionSpec as P


ITERS = 3
FRAMES = 256
VECS = 64
BLOCK = 64
SIZES = dict(x=4, z=8, y=4, core=2)
FRM = ("y", "core")
VOX = ("x", "z")
MEMBERS = SIZES["y"] * SIZES["core"]
NT = (((1,), (1,)), ((), ()))
PAIRS = [(i, j) for i in range(FRAMES // BLOCK) for j in range(i, FRAMES // BLOCK)]


def split(value):
    high = value.astype(jnp.bfloat16)
    low = (value - high.astype(jnp.float32)).astype(jnp.bfloat16)
    return high, low


def gram_kernel(place_ref, *refs):
    pieces, before_ref = refs[:MEMBERS], refs[MEMBERS]
    packed_ref, high_ref, low_ref, main, cross = refs[MEMBERS + 1 :]
    step, rows = pl.program_id(0), pieces[0].shape[0]

    @pl.when(step == 0)
    def _():
        main[...] = jnp.zeros_like(main)
        cross[...] = jnp.zeros_like(cross)

    for mask, piece_ref in enumerate(pieces):
        mine = pl.ds(pl.multiple_of((place_ref[0] ^ mask) * rows, rows), rows)
        high_ref[mine, :], low_ref[mine, :] = split(piece_ref[...])
    high, low = high_ref[...], low_ref[...]
    main[...] += lax.dot_general(high, high, NT, preferred_element_type=jnp.float32)
    cross[...] += lax.dot_general(high, low, NT, preferred_element_type=jnp.float32)

    @pl.when(step == pl.num_programs(0) - 1)
    def _():
        total = main[...] + cross[...] + cross[...].T
        packed_ref[...] = before_ref[...] + jnp.concatenate(
            [total[i * BLOCK : (i + 1) * BLOCK, j * BLOCK : (j + 1) * BLOCK] for i, j in PAIRS], axis=1
        )


def gram_packed(place, pieces, before):
    chunk = 512
    rows, width = pieces[0].shape
    packed = pl.BlockSpec((BLOCK, BLOCK * len(PAIRS)), lambda n, place: (0, 0))
    parts = pl.BlockSpec((FRAMES, chunk), lambda n, place: (0, n))
    return pl.pallas_call(
        gram_kernel,
        out_shape=(
            jax.ShapeDtypeStruct(before.shape, jnp.float32),
            jax.ShapeDtypeStruct((FRAMES, width), jnp.bfloat16),
            jax.ShapeDtypeStruct((FRAMES, width), jnp.bfloat16),
        ),
        grid_spec=pltpu.PrefetchScalarGridSpec(
            num_scalar_prefetch=1,
            grid=(width // chunk,),
            in_specs=[pl.BlockSpec((rows, chunk), lambda n, place: (0, n))] * MEMBERS + [packed],
            out_specs=(packed, parts, parts),
            scratch_shapes=[pltpu.VMEM((FRAMES, FRAMES), jnp.float32)] * 2,
        ),
        compiler_params=pltpu.CompilerParams(vmem_limit_bytes=60 << 20),
        cost_estimate=pl.CostEstimate(
            flops=2 * 3 * FRAMES * FRAMES * width, bytes_accessed=4 << 20, transcendentals=0
        ),
        name="gram",
    )(place, *pieces, before)


def image_kernel(turned_ref, high_ref, low_ref, image_ref):
    high, low = split(turned_ref[...])
    dot = functools.partial(jnp.dot, preferred_element_type=jnp.float32)
    image_ref[...] = dot(high, high_ref[...]) + (dot(high, low_ref[...]) + dot(low, high_ref[...]))


def image_of(turned, high, low):
    chunk = 512
    width = high.shape[1]
    parts = pl.BlockSpec((FRAMES, chunk), lambda n: (0, n))
    return pl.pallas_call(
        image_kernel,
        out_shape=jax.ShapeDtypeStruct((VECS, width), jnp.float32),
        grid=(width // chunk,),
        in_specs=[pl.BlockSpec((VECS, FRAMES), lambda n: (0, 0)), parts, parts],
        out_specs=pl.BlockSpec((VECS, chunk), lambda n: (0, n)),
        compiler_params=pltpu.CompilerParams(vmem_limit_bytes=8 << 20),
        cost_estimate=pl.CostEstimate(flops=2 * 3 * VECS * FRAMES * width, bytes_accessed=4 << 20, transcendentals=0),
        name="image",
    )(turned, high, low)


def inverse_factor(small):
    size = small.shape[0]
    shape = (8, 2 * size)
    sublane = lax.broadcasted_iota(jnp.int32, shape, 0)
    wide = jnp.concatenate([small, jnp.eye(size, dtype=jnp.float32)], axis=1)
    rows = [wide[8 * i : 8 * i + 8, :] for i in range(size // 8)]

    def spread_row(value, row):
        return jnp.broadcast_to(value[row : row + 1, :], shape)

    scaled = []
    for block in range(size // 8):
        held = {
            i: [jnp.broadcast_to(rows[i][:, 8 * block + t : 8 * block + t + 1], shape) for t in range(8)]
            for i in range(block, size // 8)
        }
        diagonal, mine = held[block], rows[block]
        pivots = jnp.zeros(shape, jnp.float32)
        inverses, pivot_rows, heads = [], [], []
        for t in range(8):
            pivot = spread_row(diagonal[t], t)
            pivots = jnp.where(sublane == t, pivot, pivots)
            inverse = 1.0 / pivot
            factor = jnp.where(sublane > t, diagonal[t] * inverse, 0.0)
            row = spread_row(mine, t)
            mine = mine - factor * row
            head = {}
            for j in range(t + 1, 8):
                head[j] = spread_row(diagonal[j], t)
                diagonal[j] = diagonal[j] - factor * head[j]
            inverses.append(inverse)
            pivot_rows.append(row)
            heads.append(head)
        for i in range(block + 1, size // 8):
            for t in range(8):
                factor = held[i][t] * inverses[t]
                rows[i] = rows[i] - factor * pivot_rows[t]
                for j in range(t + 1, 8):
                    held[i][j] = held[i][j] - factor * heads[t][j]
        scaled.append(mine * lax.rsqrt(pivots))
    return jnp.concatenate(scaled, axis=0)[:, size:]


def iterate_kernel(place_ref, packed_ref, start_ref, turned_ref, mine_ref, gram, vectors):
    for n, (i, j) in enumerate(PAIRS):
        block = packed_ref[:, n * BLOCK : (n + 1) * BLOCK]
        gram[i * BLOCK : (i + 1) * BLOCK, j * BLOCK : (j + 1) * BLOCK] = block
        if i != j:
            gram[j * BLOCK : (j + 1) * BLOCK, i * BLOCK : (i + 1) * BLOCK] = block.T
    dot = functools.partial(
        lax.dot_general, precision=lax.Precision.HIGHEST, preferred_element_type=jnp.float32
    )
    turned_ref[...] = start_ref[...]

    @pl.loop(0, ITERS)
    def _(step):
        projected = dot(turned_ref[...], gram[...], NT)
        small = dot(projected, projected, NT)
        turned_ref[...] = dot(inverse_factor(small), projected, (((1,), (0,)), ((), ())))

    vectors[...] = turned_ref[...].T
    rows = mine_ref.shape[0]
    mine_ref[...] = vectors[pl.ds(pl.multiple_of(place_ref[0] * rows, rows), rows), :]


def iterate(place, packed, turned, rows):
    vmem = pl.BlockSpec(memory_space=pltpu.VMEM)
    return pl.pallas_call(
        iterate_kernel,
        out_shape=(
            jax.ShapeDtypeStruct((VECS, FRAMES), jnp.float32),
            jax.ShapeDtypeStruct((rows, VECS), jnp.float32),
        ),
        in_specs=[pl.BlockSpec(memory_space=pltpu.SMEM), vmem, vmem],
        out_specs=(vmem, vmem),
        scratch_shapes=[pltpu.VMEM((FRAMES, FRAMES), jnp.float32), pltpu.VMEM((FRAMES, VECS), jnp.float32)],
        compiler_params=pltpu.CompilerParams(vmem_limit_bytes=8 << 20),
        cost_estimate=pl.CostEstimate(flops=1 << 30, bytes_accessed=1 << 20, transcendentals=0),
        name="iterate",
    )(place, packed, turned)


def exchange(value, axis, mask):
    pairs = [(2 * i + core, 2 * (i ^ mask) + 1 - core) for i in range(SIZES[axis]) for core in (0, 1)]
    return lax.ppermute(value, (axis, "core"), pairs)


def halves(value, side):
    half = value.shape[0] // 2
    low, high = value[:half], value[half:]
    return jnp.where(side == 1, high, low), jnp.where(side == 1, low, high)


def joined(value, other, side):
    return jnp.where(side == 1, jnp.concatenate([other, value]), jnp.concatenate([value, other]))


def exchanges(values, axis):
    found = [values[0]]
    for mask in (1, 2, 3):
        flip = 1 if mask != 3 else 0
        pairs = [(2 * i + core, 2 * (i ^ mask) + (core ^ flip)) for i in range(4) for core in (0, 1)]
        found.append(lax.ppermute(values[mask], (axis, "core"), pairs))
    return found


def total_of(packed):
    x, z, y, core = (lax.axis_index(axis) for axis in SIZES)
    lane = (core ^ x ^ (x >> 1) ^ z ^ (z >> 1) ^ y ^ (y >> 1)) & 1
    kept, sent = halves(packed, lane)
    value = kept + swap(sent)
    rows = value.shape[0] // 4
    parts = [lax.dynamic_slice_in_dim(value, (y ^ mask) * rows, rows, axis=0) for mask in range(4)]
    for axis, values in (("y", parts), ("x", None)):
        a, b, c, d = exchanges(values or [value] * 4, axis)
        value = (a + b) + (c + d)
    for mask in (1, 2, 6):
        value = value + exchange(value, "z", mask)
    a, b, c, d = exchanges([value] * 4, "y")
    odd, high = (y & 1) == 1, (y >> 1) == 1
    a, b, c, d = jnp.where(odd, b, a), jnp.where(odd, a, b), jnp.where(odd, d, c), jnp.where(odd, c, d)
    low, up = jnp.concatenate([a, b]), jnp.concatenate([c, d])
    value = jnp.where(high, jnp.concatenate([up, low]), jnp.concatenate([low, up]))
    return joined(value, swap(value), lane)


def subtract_kernel(offsets, place_ref, *refs):
    vectors_ref, images, casorati_ref, filtered_ref = refs[0], refs[1 : 1 + len(offsets)], refs[-2], refs[-1]
    high, low = split(vectors_ref[...])
    left = jnp.concatenate([high, high, low], axis=1)
    for n, image_ref in enumerate(images):

        @pl.when(pl.program_id(0) == n)
        def _():
            top, bottom = split(image_ref[...])
            right = jnp.concatenate([top, bottom, top], axis=0)
            filtered_ref[...] = casorati_ref[...] - jnp.dot(left, right, preferred_element_type=jnp.float32)


def subtract(place, mine, pieces, casorati, filtered):
    rows, width = casorati.shape[0], pieces[0][3].shape[1]
    halves = casorati.shape[1] // width // (SIZES["y"] * SIZES["core"])

    def column(n, place):
        found = 0
        for index, (up, other, half, _) in enumerate(pieces):
            chip = (place[0] // 2 + up) % SIZES["y"]
            core = place[0] % 2 if other == 0 else 1 - place[0] % 2
            found = jnp.where(n == index, (chip * 2 + core) * halves + half, found)
        return (0, found)

    block = pl.BlockSpec((rows, width), column)
    specs = [pl.BlockSpec((rows, VECS), lambda n, place: (0, 0))]
    specs += [pl.BlockSpec((VECS, width), lambda n, place: (0, 0))] * len(pieces)
    operands = [mine, *[piece[3] for piece in pieces]]
    aliases = {}
    if filtered is not None:
        aliases = {1 + len(operands): 0}
        specs.append(pl.BlockSpec(memory_space=pl.ANY))
        operands.append(filtered)
    specs.append(block)
    operands.append(casorati)
    return pl.pallas_call(
        functools.partial(subtract_kernel, pieces),
        out_shape=jax.ShapeDtypeStruct(casorati.shape, jnp.float32),
        grid_spec=pltpu.PrefetchScalarGridSpec(
            num_scalar_prefetch=1, grid=(len(pieces),), in_specs=specs, out_specs=block
        ),
        input_output_aliases=aliases,
        compiler_params=pltpu.CompilerParams(vmem_limit_bytes=12 << 20),
        cost_estimate=pl.CostEstimate(
            flops=2 * 6 * VECS * rows * width * len(pieces), bytes_accessed=len(pieces) << 20, transcendentals=0
        ),
        name="subtract",
    )(place, *operands)


def shift(value, step):
    return lax.ppermute(value, "y", [(i, (i + step) % SIZES["y"]) for i in range(SIZES["y"])])


def swap(value):
    return lax.ppermute(value, "core", [(0, 1), (1, 0)])


def body(casorati, start):
    index = lax.axis_index(FRM)
    place = index.reshape(1)
    rows, width = casorati.shape[0], casorati.shape[1] // MEMBERS // 2
    packed = jnp.zeros((BLOCK, BLOCK * len(PAIRS)), jnp.float32)
    halved = []
    gathered = []
    for half in range(2):
        pieces = []
        for mask in range(MEMBERS):
            piece = lax.dynamic_slice(casorati, (0, ((index ^ mask) * 2 + half) * width), (rows, width))
            if mask:
                piece = lax.ppermute(piece, FRM, [(i, i ^ mask) for i in range(MEMBERS)])
            pieces.append(piece)
        gathered.append(pieces)
    for pieces in gathered:
        packed, *parts = gram_packed(place, pieces, packed)
        halved.append(parts)
    turned, mine = iterate(place, total_of(packed), start.T, rows)
    left, right = (image_of(turned, *parts) for parts in halved)

    up_left, down_right = shift(left, 1), shift(right, -1)
    up_right, down_left = shift(right, 1), shift(left, -1)
    far_left, far_right = shift(up_left, 1), shift(down_right, -1)
    groups = {
        "near": [(0, 0, left), (0, 1, right)],
        "first": [(-1, 0, up_left), (1, 1, down_right)],
        "second": [(-1, 1, up_right), (1, 0, down_left)],
        "far": [(2, 0, far_left), (2, 1, far_right)],
    }
    filtered = None
    for parts in groups.values():
        pieces = [(up, 0, side, value) for up, side, value in parts]
        pieces += [(up, 1, side, swap(value)) for up, side, value in parts]
        filtered = subtract(place, mine, pieces, casorati, filtered)
    return turned.T, filtered


def solution(mesh):
    inner = Mesh(mesh.devices.reshape(4, 8, 4, 2), tuple(SIZES))
    return jax.shard_map(
        body,
        mesh=inner,
        in_specs=(P(FRM, VOX), P()),
        out_specs=(P(), P(FRM, VOX)),
        check_vma=False,
    )
```

time: 198 us -> 177 us (0.89)
  blocking collectives: 55.1 us -> 0 us
  waiting for transfers between devices: 47.6 us -> 70.1 us
  starting transfers between devices: 50.7 us -> 65.3 us
  matrix products: 3.67 us -> 0 us
    all_to_all x1 -> x0, blocking collectives: 55.1 us -> none  [body(): lax.all_to_all(casorati, FRM, split_axis=1, concat_axis=0, tiled=True)]
    ppermute x2 -> x23, waiting for transfers between devices: 2.44 us -> 37.5 us  [the longest x14 29.4 us: body(): piece = lax.ppermute(piece, FRM, [(i, i ^ mask) for i in range(MEMBERS)])]
    ppermute x2 -> x23, starting transfers between devices: 2.58 us -> 36.8 us  [the longest x14 23.6 us: body(): piece = lax.ppermute(piece, FRM, [(i, i ^ mask) for i in range(MEMBERS)])]
    ppermute x9 -> x3, starting transfers between devices: 31 us -> 12.7 us  [exchange(): return lax.ppermute(value, (axis, 'core'), pairs)]
    ppermute x9 -> x3, waiting for transfers between devices: 20.9 us -> 4.4 us  [exchange(): return lax.ppermute(value, (axis, 'core'), pairs)]
    dot_general x1 -> x0, matrix products: 3.67 us -> none  [body(): lax.dot_general(turned, columns, (((1,), (0,)), ((), ())), precision=lax....]
    dynamic_slice x1 -> x2, local copies, waits for them, and re-layouts: 0.6 us -> 3.32 us  [the longest x1 3.3 us: body(): lax.dynamic_slice(casorati, (0, ((index ^ mask) * 2 + half) * width), (ro...]
    all_to_all x1 -> x0, local copies, waits for them, and re-layouts: 2.47 us -> none  [body(): lax.all_to_all(casorati, FRM, split_axis=1, concat_axis=0, tiled=True)]
  transfers between devices with their start and end apart: 25 -> 42, of which waited for: 15 -> 22; matrix products, arithmetic and copies ran while one was open for 1% -> 0% of each run, Pallas kernels for 0% -> 8%
where the time goes in v2:
time: 177 us; the launch traced here: 176 us
  waiting for transfers between devices  70.1 us (40%)
  starting transfers between devices  65.3 us (37%)
  Pallas kernels  32.3 us (18%)
  local copies, waits for them, and re-layouts  5.56 us (3%)
  other arithmetic  2.1 us (1%)
    ppermute x14, waiting for transfers between devices, body(): piece = lax.ppermute(piece, FRM, [(i, i ^ mask) for i in range(MEMBERS)])  29.4 us
    ppermute x6, waiting for transfers between devices, shift(): lax.ppermute(value, 'y', [(i, (i + step) % SIZES['y']) for i in range(SIZ...  25.7 us
    ppermute x14, starting transfers between devices, body(): piece = lax.ppermute(piece, FRM, [(i, i ^ mask) for i in range(MEMBERS)])  23.6 us
    ppermute x9, starting transfers between devices, exchanges(): found.append(lax.ppermute(values[mask], (axis, 'core'), pairs))  13.2 us
    ppermute x3, starting transfers between devices, exchange(): return lax.ppermute(value, (axis, 'core'), pairs)  12.7 us
    pallas_call x4, Pallas kernels, subtract(): pl.pallas_call(functools.partial(subtract_kernel, pieces), out_shape=jax....  10.4 us
    pallas_call x2, Pallas kernels, gram_packed(): pl.pallas_call(gram_kernel, out_shape=(jax.ShapeDtypeStruct(before.shape,...  10.2 us
    pallas_call x1, Pallas kernels, iterate(): pl.pallas_call(iterate_kernel, out_shape=(jax.ShapeDtypeStruct((VECS, FRA...  9.17 us
  transfers between devices with their start and end apart: 42, of which 22 were waited for; matrix products, arithmetic and copies ran while one was open for 0% of the time, Pallas kernels for 8%

profile of v2, /device:TPU:1, one launch (start us, length us, event | category | flops | bytes accessed | tf_op | source)
XLA Modules:
  0.0 176.3 jit_solution(17702868054493950699)
XLA Ops:
  0.7 3.3 %constant_dynamic-slice_fusion.3 = (f32[32,2048]{1,0:T(8,128)S(1)}, f32[32,2048]{1,0:T(8,128)S(1)}, f32[32,2048]{1,0:T(8,128)S(1)}, f32[32,2048]{1,0:T(8,128)S(1...) fusion(f32[32,32768]{1,0:T(8,128)} %refs_6_.5, ...), kind=kLoop, calls=%fused_computation.13 | loop fusion | bytes 8388672 | tf_op jit(solution)/shard_map/dynamic_slice | solution.py:299
  4.0 3.8 %collective-permute-start.10 = (f32[32,2048]{1,0:T(8,128)S(1)}, f32[32,2048]{1,0:T(8,128)S(1)}, u32[]{:S(2)}, u32[]{:S(2)}) collective-permute-start(f32[32,2048]{1,0:T(8,128)S(1)} %get-tuple-element.21), channel_id=1, source_target_pairs={{0,4},{1,5},{2,6},{3,7},{4,0},{5,1},{6,2},{7,3},{8,12},{9,13},{10,... | collective-permute-start | bytes 786440 | tf_op jit(solution)/shard_map/ppermute | solution.py:301
  7.8 2.6 %collective-permute-start.11 = (f32[32,2048]{1,0:T(8,128)S(1)}, f32[32,2048]{1,0:T(8,128)S(1)}, u32[]{:S(2)}, u32[]{:S(2)}) collective-permute-start(f32[32,2048]{1,0:T(8,128)S(1)} %get-tuple-element.20), channel_id=1, source_target_pairs={{0,5},{1,4},{2,7},{3,6},{4,1},{5,0},{6,3},{7,2},{8,13},{9,12},{10,... | collective-permute-start | bytes 786440 | tf_op jit(solution)/shard_map/ppermute | solution.py:301
  11.6 1.9 %collective-permute-start.7 = (f32[32,2048]{1,0:T(8,128)S(1)}, f32[32,2048]{1,0:T(8,128)S(1)}, u32[]{:S(2)}, u32[]{:S(2)}) collective-permute-start(f32[32,2048]{1,0:T(8,128)S(1)} %get-tuple-element.24), channel_id=1, source_target_pairs={{0,1},{1,0},{2,3},{3,2},{4,5},{5,4},{6,7},{7,6},{8,9},{9,8},{10,11... | collective-permute-start | bytes 786440 | tf_op jit(solution)/shard_map/ppermute | solution.py:301
  13.5 1.4 collective-permute-start.8
  14.9 6.9 %collective-permute-done.11.refs_5_ = f32[32,2048]{1,0:T(8,128)S(1)} collective-permute-done((f32[32,2048]{1,0:T(8,128)S(1)}, f32[32,2048]{1,0:T(8,128)S(1)}, u32[]{:S(2)}, u32[]{:S(2)}) %collective-permute-start.11) | collective-permute-done | bytes 262176 | tf_op jit(solution)/shard_map/ppermute | solution.py:301
  21.8 4.1 %collective-permute-done.12.refs_6_ = f32[32,2048]{1,0:T(8,128)S(1)} collective-permute-done((f32[32,2048]{1,0:T(8,128)S(1)}, f32[32,2048]{1,0:T(8,128)S(1)}, u32[]{:S(2)}, u32[]{:S(2)}) %collective-permute-start.12) | collective-permute-done | bytes 262176 | tf_op jit(solution)/shard_map/ppermute | solution.py:301
  26.3 5.2 %collective-permute-done.13.refs_7_ = f32[32,2048]{1,0:T(8,128)S(1)} collective-permute-done((f32[32,2048]{1,0:T(8,128)S(1)}, f32[32,2048]{1,0:T(8,128)S(1)}, u32[]{:S(2)}, u32[]{:S(2)}) %collective-permute-start.13) | collective-permute-done | bytes 262176 | tf_op jit(solution)/shard_map/ppermute | solution.py:301
  31.5 1.4 collective-permute-start.1
  33.7 2.9 %collective-permute-start.3 = (f32[32,2048]{1,0:T(8,128)S(1)}, f32[32,2048]{1,0:T(8,128)S(1)}, u32[]{:S(2)}, u32[]{:S(2)}) collective-permute-start(f32[32,2048]{1,0:T(8,128)S(1)} %get-tuple-element.29), channel_id=1, source_target_pairs={{0,4},{1,5},{2,6},{3,7},{4,0},{5,1},{6,2},{7,3},{8,12},{9,13},{10,... | collective-permute-start | bytes 786440 | tf_op jit(solution)/shard_map/ppermute | solution.py:301
  36.8 2.5 %collective-permute-start.5 = (f32[32,2048]{1,0:T(8,128)S(1)}, f32[32,2048]{1,0:T(8,128)S(1)}, u32[]{:S(2)}, u32[]{:S(2)}) collective-permute-start(f32[32,2048]{1,0:T(8,128)S(1)} %get-tuple-element.27), channel_id=1, source_target_pairs={{0,6},{1,7},{2,4},{3,5},{4,2},{5,3},{6,0},{7,1},{8,14},{9,15},{10,... | collective-permute-start | bytes 786440 | tf_op jit(solution)/shard_map/ppermute | solution.py:301
  39.4 4.5 %collective-permute-start.6 = (f32[32,2048]{1,0:T(8,128)S(1)}, f32[32,2048]{1,0:T(8,128)S(1)}, u32[]{:S(2)}, u32[]{:S(2)}) collective-permute-start(f32[32,2048]{1,0:T(8,128)S(1)} %get-tuple-element.26), channel_id=1, source_target_pairs={{0,7},{1,6},{2,5},{3,4},{4,3},{5,2},{6,1},{7,0},{8,15},{9,14},{10,... | collective-permute-start | bytes 786440 | tf_op jit(solution)/shard_map/ppermute | solution.py:301
  44.6 5.1 %gram.2 = (f32[64,640]{1,0:T(8,128)}, bf16[256,2048]{1,0:T(8,128)(2,1)}, bf16[256,2048]{1,0:T(8,128)(2,1)}) custom-call(s32[1]{0:T(128)} %bitcast.place_ref, f32[32,2048]{1,0:T(8,128)} %get-tuple-element.25.refs_0_, f32[32,2048]{1,0:T(8,128)} %copy-done.12, f32[32,2048]{1,0:T(8,128)} %copy-done.14, f32[32,2048]{1,0:T(8,128)} %copy-done.16, ...), custom_call_target="tpu_custom_call" | custom-call | flops 805306368 | bytes 4194304 | tf_op jit(solution)/shard_map/gram/pallas_call | solution.py:60
  49.7 3.1 %collective-permute-done.3.refs_4_ = f32[32,2048]{1,0:T(8,128)S(1)} collective-permute-done((f32[32,2048]{1,0:T(8,128)S(1)}, f32[32,2048]{1,0:T(8,128)S(1)}, u32[]{:S(2)}, u32[]{:S(2)}) %collective-permute-start.3) | collective-permute-done | bytes 262176 | tf_op jit(solution)/shard_map/ppermute | solution.py:301
  52.8 6.2 %collective-permute-done.4.refs_5_ = f32[32,2048]{1,0:T(8,128)S(1)} collective-permute-done((f32[32,2048]{1,0:T(8,128)S(1)}, f32[32,2048]{1,0:T(8,128)S(1)}, u32[]{:S(2)}, u32[]{:S(2)}) %collective-permute-start.4) | collective-permute-done | bytes 262176 | tf_op jit(solution)/shard_map/ppermute | solution.py:301
  59.0 3.9 %collective-permute-done.6.refs_7_ = f32[32,2048]{1,0:T(8,128)S(1)} collective-permute-done((f32[32,2048]{1,0:T(8,128)S(1)}, f32[32,2048]{1,0:T(8,128)S(1)}, u32[]{:S(2)}, u32[]{:S(2)}) %collective-permute-start.6) | collective-permute-done | bytes 262176 | tf_op jit(solution)/shard_map/ppermute | solution.py:301
  63.6 5.1 %gram.3 = (f32[64,640]{1,0:T(8,128)}, bf16[256,2048]{1,0:T(8,128)(2,1)}, bf16[256,2048]{1,0:T(8,128)(2,1)}) custom-call(s32[1]{0:T(128)} %bitcast.place_ref, f32[32,2048]{1,0:T(8,128)} %get-tuple-element.33.refs_0_, f32[32,2048]{1,0:T(8,128)} %copy-done.10, f32[32,2048]{1,0:T(8,128)} %copy-done.13, f32[32,2048]{1,0:T(8,128)} %copy-done.15, ...), custom_call_target="tpu_custom_call" | custom-call | flops 805306368 | bytes 4194304 | tf_op jit(solution)/shard_map/gram/pallas_call | solution.py:60
  70.0 1.2 collective-permute-done.14
  72.3 4.0 %collective-permute-start.16 = (f32[8,640]{1,0:T(8,128)S(1)}, f32[8,640]{1,0:T(8,128)S(1)}, u32[]{:S(2)}, u32[]{:S(2)}) collective-permute-start(f32[8,640]{1,0:T(8,128)S(1)} %get-tuple-element.36), channel_id=1, source_target_pairs={{0,5},{1,4},{2,7},{3,6},{4,1},{5,0},{6,3},{7,2},{8,13},{9,12},{10,... | collective-permute-start | bytes 61448 | tf_op jit(solution)/shard_map/ppermute | solution.py:206
  76.4 1.5 collective-permute-done.16
  77.9 2.2 %collective-permute-done.17 = f32[8,640]{1,0:T(8,128)S(1)} collective-permute-done((f32[8,640]{1,0:T(8,128)S(1)}, f32[8,640]{1,0:T(8,128)S(1)}, u32[]{:S(2)}, u32[]{:S(2)}) %collective-permute-start.17) | collective-permute-done | bytes 20512 | tf_op jit(solution)/shard_map/ppermute | solution.py:206
  80.1 2.7 %collective-permute-start.18 = (f32[8,640]{1,0:T(8,128)S(1)}, f32[8,640]{1,0:T(8,128)S(1)}, u32[]{:S(2)}, u32[]{:S(2)}) collective-permute-start(f32[8,640]{1,0:T(8,128)S(1)} %add_add_fusion.1), channel_id=1, source_target_pairs={{0,65},{1,64},{64,1},{65,0},{128,193},{129,192},{192,129},{193,128... | collective-permute-start | bytes 61448 | tf_op jit(solution)/shard_map/ppermute | solution.py:206
  82.8 1.6 collective-permute-start.19
  85.3 2.2 %collective-permute-done.19 = f32[8,640]{1,0:T(8,128)S(1)} collective-permute-done((f32[8,640]{1,0:T(8,128)S(1)}, f32[8,640]{1,0:T(8,128)S(1)}, u32[]{:S(2)}, u32[]{:S(2)}) %collective-permute-start.19) | collective-permute-done | bytes 20512 | tf_op jit(solution)/shard_map/ppermute | solution.py:206
  88.2 4.0 %collective-permute-start.21 = (f32[8,640]{1,0:T(8,128)S(1)}, f32[8,640]{1,0:T(8,128)S(1)}, u32[]{:S(2)}, u32[]{:S(2)}) collective-permute-start(f32[8,640]{1,0:T(8,128)S(1)} %add_add_fusion), channel_id=1, source_target_pairs={{0,9},{1,8},{8,1},{9,0},{16,25},{17,24},{24,17},{25,16},{32,41},{3... | collective-permute-start | bytes 61448 | tf_op jit(solution)/shard_map/ppermute | solution.py:188
  92.2 1.5 collective-permute-done.21
  93.7 3.1 %collective-permute-start.22 = (f32[8,640]{1,0:T(8,128)S(1)}, f32[8,640]{1,0:T(8,128)S(1)}, u32[]{:S(2)}, u32[]{:S(2)}) collective-permute-start(f32[8,640]{1,0:T(8,128)S(1)} %add.153), channel_id=1, source_target_pairs={{0,17},{1,16},{8,25},{9,24},{16,1},{17,0},{24,9},{25,8},{32,49},{3... | collective-permute-start | bytes 61448 | tf_op jit(solution)/shard_map/ppermute | solution.py:188
  96.8 1.5 collective-permute-done.22
  98.2 5.7 %collective-permute-start.23 = (f32[8,640]{1,0:T(8,128)S(1)}, f32[8,640]{1,0:T(8,128)S(1)}, u32[]{:S(2)}, u32[]{:S(2)}) collective-permute-start(f32[8,640]{1,0:T(8,128)S(1)} %add.154), channel_id=1, source_target_pairs={{0,49},{1,48},{8,57},{9,56},{16,33},{17,32},{24,41},{25,40},{32,17... | collective-permute-start | bytes 61448 | tf_op jit(solution)/shard_map/ppermute | solution.py:188
  103.9 1.5 collective-permute-done.23
  105.7 3.6 %collective-permute-start.25 = (f32[8,640]{1,0:T(8,128)S(1)}, f32[8,640]{1,0:T(8,128)S(1)}, u32[]{:S(2)}, u32[]{:S(2)}) collective-permute-start(f32[8,640]{1,0:T(8,128)S(1)} %add.155), channel_id=1, source_target_pairs={{0,5},{1,4},{2,7},{3,6},{4,1},{5,0},{6,3},{7,2},{8,13},{9,12},{10,... | collective-permute-start | bytes 61448 | tf_op jit(solution)/shard_map/ppermute | solution.py:206
  112.1 9.2 %iterate.1 = (f32[64,256]{1,0:T(8,128)}, f32[32,64]{1,0:T(8,128)S(1)}) custom-call(s32[1]{0:T(128)} %bitcast.place_ref, f32[64,640]{1,0:T(8,128)S(1)} %maximum_select_fusion.packed_ref, f32[64,256]{1,0:T(8,128)S(1)} %bitcast.4), custom_call_target="tpu_custom_call" | custom-call | flops 1073741824 | bytes 1048576 | tf_op jit(solution)/shard_map/iterate/pallas_call | solution.py:171
  122.1 1.3 image.3.refs_2_
  123.6 2.2 %collective-permute-start.30 = (f32[64,2048]{1,0:T(8,128)S(1)}, f32[64,2048]{1,0:T(8,128)S(1)}, u32[]{:S(2)}, u32[]{:S(2)}) collective-permute-start(f32[64,2048]{1,0:T(8,128)S(1)} %image.3.refs_2_), channel_id=1, source_target_pairs={{0,6},{2,0},{4,2},{6,4},{1,7},{3,1},{5,3},{7,5},{8,14},{10,8},{12,... | collective-permute-start | bytes 1572872 | tf_op jit(solution)/shard_map/ppermute | solution.py:282
  125.9 1.3 image.2.refs_1_
  128.1 2.5 %collective-permute-start.35 = (f32[64,2048]{1,0:T(8,128)S(1)}, f32[64,2048]{1,0:T(8,128)S(1)}, u32[]{:S(2)}, u32[]{:S(2)}) collective-permute-start(f32[64,2048]{1,0:T(8,128)S(1)} %image.2.refs_1_), channel_id=1, source_target_pairs={{0,6},{2,0},{4,2},{6,4},{1,7},{3,1},{5,3},{7,5},{8,14},{10,8},{12,... | collective-permute-start | bytes 1572872 | tf_op jit(solution)/shard_map/ppermute | solution.py:282
  130.6 6.2 %collective-permute-done.30.refs_2_ = f32[64,2048]{1,0:T(8,128)S(1)} collective-permute-done((f32[64,2048]{1,0:T(8,128)S(1)}, f32[64,2048]{1,0:T(8,128)S(1)}, u32[]{:S(2)}, u32[]{:S(2)}) %collective-permute-start.30) | collective-permute-done | bytes 524320 | tf_op jit(solution)/shard_map/ppermute | solution.py:282
  136.8 2.0 %collective-permute-start.39 = (f32[64,2048]{1,0:T(8,128)S(1)}, f32[64,2048]{1,0:T(8,128)S(1)}, u32[]{:S(2)}, u32[]{:S(2)}) collective-permute-start(f32[64,2048]{1,0:T(8,128)S(1)} %collective-permute-done.30.refs_2_), channel_id=1, source_target_pairs={{0,1},{1,0},{2,3},{3,2},{4,5},{5,4},{6,7},{7,6},{8,9},{9,8},{10,11... | collective-permute-start | bytes 1572872 | tf_op jit(solution)/shard_map/ppermute | solution.py:286
  138.8 3.4 %collective-permute-start.31 = (f32[64,2048]{1,0:T(8,128)S(1)}, f32[64,2048]{1,0:T(8,128)S(1)}, u32[]{:S(2)}, u32[]{:S(2)}) collective-permute-start(f32[64,2048]{1,0:T(8,128)S(1)} %collective-permute-done.30.refs_2_), channel_id=1, source_target_pairs={{0,6},{2,0},{4,2},{6,4},{1,7},{3,1},{5,3},{7,5},{8,14},{10,8},{12,... | collective-permute-start | bytes 1572872 | tf_op jit(solution)/shard_map/ppermute | solution.py:282
  142.5 11.2 %collective-permute-done.34.refs_1_ = f32[64,2048]{1,0:T(8,128)S(1)} collective-permute-done((f32[64,2048]{1,0:T(8,128)S(1)}, f32[64,2048]{1,0:T(8,128)S(1)}, u32[]{:S(2)}, u32[]{:S(2)}) %collective-permute-start.34) | collective-permute-done | bytes 524320 | tf_op jit(solution)/shard_map/ppermute | solution.py:282
  153.7 1.5 collective-permute-start.38
  155.7 3.5 %collective-permute-done.31.refs_2_ = f32[64,2048]{1,0:T(8,128)S(1)} collective-permute-done((f32[64,2048]{1,0:T(8,128)S(1)}, f32[64,2048]{1,0:T(8,128)S(1)}, u32[]{:S(2)}, u32[]{:S(2)}) %collective-permute-start.31) | collective-permute-done | bytes 524320 | tf_op jit(solution)/shard_map/ppermute | solution.py:282
  159.2 1.2 collective-permute-start.33
  160.5 4.5 %collective-permute-done.29.refs_1_ = f32[64,2048]{1,0:T(8,128)S(1)} collective-permute-done((f32[64,2048]{1,0:T(8,128)S(1)}, f32[64,2048]{1,0:T(8,128)S(1)}, u32[]{:S(2)}, u32[]{:S(2)}) %collective-permute-start.29) | collective-permute-done | bytes 524320 | tf_op jit(solution)/shard_map/ppermute | solution.py:282
  165.9 2.6 %subtract.4.refs_5_ = f32[32,32768]{1,0:T(8,128)} custom-call(s32[1]{0:T(128)} %bitcast.place_ref, f32[32,64]{1,0:T(8,128)S(1)} %get-tuple-element.13.refs_0_, f32[64,2048]{1,0:T(8,128)S(1)} %image.2.refs_1_, f32[64,2048]{1,0:T(8,128)S(1)} %image.3.refs_2_, f32[64,2048]{1,0:T(8,128)S(1)} %collective-permute-done.40.refs_3_, ...), custom_call_target="tpu_custom_call" | custom-call | flops 201326592 | bytes 4194304 | tf_op jit(solution)/shard_map/subtract/pallas_call | solution.py:266
  168.4 2.6 %subtract.5.refs_5_ = f32[32,32768]{1,0:T(8,128)} custom-call(s32[1]{0:T(128)} %bitcast.place_ref, f32[32,64]{1,0:T(8,128)S(1)} %get-tuple-element.13.refs_0_, f32[64,2048]{1,0:T(8,128)S(1)} %collective-permute-done.28.refs_1_, f32[64,2048]{1,0:T(8,128)S(1)} %collective-permute-done.30.refs_2_, ...), custom_call_target="tpu_custom_call", output_to_operand_aliasing={{}: (6, {})} | custom-call | flops 201326592 | bytes 4194304 | tf_op jit(solution)/shard_map/subtract/pallas_call | solution.py:266
  171.0 2.6 %subtract.6.refs_5_ = f32[32,32768]{1,0:T(8,128)} custom-call(s32[1]{0:T(128)} %bitcast.place_ref, f32[32,64]{1,0:T(8,128)S(1)} %get-tuple-element.13.refs_0_, f32[64,2048]{1,0:T(8,128)S(1)} %collective-permute-done.34.refs_1_, f32[64,2048]{1,0:T(8,128)S(1)} %collective-permute-done.35.refs_2_, ...), custom_call_target="tpu_custom_call", output_to_operand_aliasing={{}: (6, {})} | custom-call | flops 201326592 | bytes 4194304 | tf_op jit(solution)/shard_map/subtract/pallas_call | solution.py:266
  173.7 2.6 %subtract.7 = f32[32,32768]{1,0:T(8,128)} custom-call(s32[1]{0:T(128)} %bitcast.place_ref, f32[32,64]{1,0:T(8,128)S(1)} %get-tuple-element.13.refs_0_, f32[64,2048]{1,0:T(8,128)S(1)} %collective-permute-done.29.refs_1_, f32[64,2048]{1,0:T(8,128)S(1)} %collective-permute-done.31.refs_2_, ...), custom_call_target="tpu_custom_call", output_to_operand_aliasing={{}: (6, {})} | custom-call | flops 201326592 | bytes 4194304 | tf_op jit(solution)/shard_map/subtract/pallas_call | solution.py:266
  (101 shorter events, 14.9 us)
Async XLA Ops:
  4.0 108.1 %copy-start.6 = (f32[256,64]{0,1:T(8,128)S(1)}, f32[256,64]{0,1:T(8,128)}, u32[]{:S(2)}) copy-start(f32[256,64]{0,1:T(8,128)} %param.3) | copy-start | bytes 196612
  4.0 9.5 %collective-permute-start.10 = (f32[32,2048]{1,0:T(8,128)S(1)}, f32[32,2048]{1,0:T(8,128)S(1)}, u32[]{:S(2)}, u32[]{:S(2)}) collective-permute-start(f32[32,2048]{1,0:T(8,128)S(1)} %get-tuple-element.21), channel_id=1, source_target_pairs={{0,4},{1,5},{2,6},{3,7},{4,0},{5,1},{6,2},{7,3},{8,12},{9,13},{10,... | collective-permute-start | bytes 786440 | tf_op jit(solution)/shard_map/ppermute | solution.py:301
  7.8 14.0 %collective-permute-start.11 = (f32[32,2048]{1,0:T(8,128)S(1)}, f32[32,2048]{1,0:T(8,128)S(1)}, u32[]{:S(2)}, u32[]{:S(2)}) collective-permute-start(f32[32,2048]{1,0:T(8,128)S(1)} %get-tuple-element.20), channel_id=1, source_target_pairs={{0,5},{1,4},{2,7},{3,6},{4,1},{5,0},{6,3},{7,2},{8,13},{9,12},{10,... | collective-permute-start | bytes 786440 | tf_op jit(solution)/shard_map/ppermute | solution.py:301
  10.4 15.5 %collective-permute-start.12 = (f32[32,2048]{1,0:T(8,128)S(1)}, f32[32,2048]{1,0:T(8,128)S(1)}, u32[]{:S(2)}, u32[]{:S(2)}) collective-permute-start(f32[32,2048]{1,0:T(8,128)S(1)} %get-tuple-element.19), channel_id=1, source_target_pairs={{0,6},{1,7},{2,4},{3,5},{4,2},{5,3},{6,0},{7,1},{8,14},{9,15},{10,... | collective-permute-start | bytes 786440 | tf_op jit(solution)/shard_map/ppermute | solution.py:301
  11.4 20.1 %collective-permute-start.13 = (f32[32,2048]{1,0:T(8,128)S(1)}, f32[32,2048]{1,0:T(8,128)S(1)}, u32[]{:S(2)}, u32[]{:S(2)}) collective-permute-start(f32[32,2048]{1,0:T(8,128)S(1)} %get-tuple-element.18), channel_id=1, source_target_pairs={{0,7},{1,6},{2,5},{3,4},{4,3},{5,2},{6,1},{7,0},{8,15},{9,14},{10,... | collective-permute-start | bytes 786440 | tf_op jit(solution)/shard_map/ppermute | solution.py:301
  11.6 21.3 %collective-permute-start.7 = (f32[32,2048]{1,0:T(8,128)S(1)}, f32[32,2048]{1,0:T(8,128)S(1)}, u32[]{:S(2)}, u32[]{:S(2)}) collective-permute-start(f32[32,2048]{1,0:T(8,128)S(1)} %get-tuple-element.24), channel_id=1, source_target_pairs={{0,1},{1,0},{2,3},{3,2},{4,5},{5,4},{6,7},{7,6},{8,9},{9,8},{10,11... | collective-permute-start | bytes 786440 | tf_op jit(solution)/shard_map/ppermute | solution.py:301
  13.5 31.1 %copy-start.7 = (f32[32,2048]{1,0:T(8,128)}, f32[32,2048]{1,0:T(8,128)S(1)}, u32[]{:S(2)}) copy-start(f32[32,2048]{1,0:T(8,128)S(1)} %collective-permute-done.10.refs_4_) | copy-start | bytes 786436
  13.5 20.2 %collective-permute-start.8 = (f32[32,2048]{1,0:T(8,128)S(1)}, f32[32,2048]{1,0:T(8,128)S(1)}, u32[]{:S(2)}, u32[]{:S(2)}) collective-permute-start(f32[32,2048]{1,0:T(8,128)S(1)} %get-tuple-element.23), channel_id=1, source_target_pairs={{0,2},{1,3},{2,0},{3,1},{4,6},{5,7},{6,4},{7,5},{8,10},{9,11},{10,... | collective-permute-start | bytes 786440 | tf_op jit(solution)/shard_map/ppermute | solution.py:301
  21.8 14.7 %collective-permute-start.9 = (f32[32,2048]{1,0:T(8,128)S(1)}, f32[32,2048]{1,0:T(8,128)S(1)}, u32[]{:S(2)}, u32[]{:S(2)}) collective-permute-start(f32[32,2048]{1,0:T(8,128)S(1)} %get-tuple-element.22), channel_id=1, source_target_pairs={{0,3},{1,2},{2,1},{3,0},{4,7},{5,6},{6,5},{7,4},{8,11},{9,10},{10,... | collective-permute-start | bytes 786440 | tf_op jit(solution)/shard_map/ppermute | solution.py:301
  25.9 10.9 %collective-permute-start = (f32[32,2048]{1,0:T(8,128)S(1)}, f32[32,2048]{1,0:T(8,128)S(1)}, u32[]{:S(2)}, u32[]{:S(2)}) collective-permute-start(f32[32,2048]{1,0:T(8,128)S(1)} %get-tuple-element.32), channel_id=1, source_target_pairs={{0,1},{1,0},{2,3},{3,2},{4,5},{5,4},{6,7},{7,6},{8,9},{9,8},{10,11... | collective-permute-start | bytes 786440 | tf_op jit(solution)/shard_map/ppermute | solution.py:301
  31.5 7.8 %collective-permute-start.1 = (f32[32,2048]{1,0:T(8,128)S(1)}, f32[32,2048]{1,0:T(8,128)S(1)}, u32[]{:S(2)}, u32[]{:S(2)}) collective-permute-start(f32[32,2048]{1,0:T(8,128)S(1)} %get-tuple-element.31), channel_id=1, source_target_pairs={{0,2},{1,3},{2,0},{3,1},{4,6},{5,7},{6,4},{7,5},{8,10},{9,11},{10,... | collective-permute-start | bytes 786440 | tf_op jit(solution)/shard_map/ppermute | solution.py:301
  32.9 16.8 %collective-permute-start.2 = (f32[32,2048]{1,0:T(8,128)S(1)}, f32[32,2048]{1,0:T(8,128)S(1)}, u32[]{:S(2)}, u32[]{:S(2)}) collective-permute-start(f32[32,2048]{1,0:T(8,128)S(1)} %get-tuple-element.30), channel_id=1, source_target_pairs={{0,3},{1,2},{2,1},{3,0},{4,7},{5,6},{6,5},{7,4},{8,11},{9,10},{10,... | collective-permute-start | bytes 786440 | tf_op jit(solution)/shard_map/ppermute | solution.py:301
  33.7 19.1 %collective-permute-start.3 = (f32[32,2048]{1,0:T(8,128)S(1)}, f32[32,2048]{1,0:T(8,128)S(1)}, u32[]{:S(2)}, u32[]{:S(2)}) collective-permute-start(f32[32,2048]{1,0:T(8,128)S(1)} %get-tuple-element.29), channel_id=1, source_target_pairs={{0,4},{1,5},{2,6},{3,7},{4,0},{5,1},{6,2},{7,3},{8,12},{9,13},{10,... | collective-permute-start | bytes 786440 | tf_op jit(solution)/shard_map/ppermute | solution.py:301
  36.5 22.5 %collective-permute-start.4 = (f32[32,2048]{1,0:T(8,128)S(1)}, f32[32,2048]{1,0:T(8,128)S(1)}, u32[]{:S(2)}, u32[]{:S(2)}) collective-permute-start(f32[32,2048]{1,0:T(8,128)S(1)} %get-tuple-element.28), channel_id=1, source_target_pairs={{0,5},{1,4},{2,7},{3,6},{4,1},{5,0},{6,3},{7,2},{8,13},{9,12},{10,... | collective-permute-start | bytes 786440 | tf_op jit(solution)/shard_map/ppermute | solution.py:301
  36.8 22.2 %collective-permute-start.5 = (f32[32,2048]{1,0:T(8,128)S(1)}, f32[32,2048]{1,0:T(8,128)S(1)}, u32[]{:S(2)}, u32[]{:S(2)}) collective-permute-start(f32[32,2048]{1,0:T(8,128)S(1)} %get-tuple-element.27), channel_id=1, source_target_pairs={{0,6},{1,7},{2,4},{3,5},{4,2},{5,3},{6,0},{7,1},{8,14},{9,15},{10,... | collective-permute-start | bytes 786440 | tf_op jit(solution)/shard_map/ppermute | solution.py:301
  39.4 23.5 %collective-permute-start.6 = (f32[32,2048]{1,0:T(8,128)S(1)}, f32[32,2048]{1,0:T(8,128)S(1)}, u32[]{:S(2)}, u32[]{:S(2)}) collective-permute-start(f32[32,2048]{1,0:T(8,128)S(1)} %get-tuple-element.26), channel_id=1, source_target_pairs={{0,7},{1,6},{2,5},{3,4},{4,3},{5,2},{6,1},{7,0},{8,15},{9,14},{10,... | collective-permute-start | bytes 786440 | tf_op jit(solution)/shard_map/ppermute | solution.py:301
  68.7 52.6 %copy-start.3 = (bf16[256,2048]{1,0:T(8,128)(2,1)S(1)}, bf16[256,2048]{1,0:T(8,128)(2,1)}, u32[]{:S(2)}) copy-start(bf16[256,2048]{1,0:T(8,128)(2,1)} %get-tuple-element.16.high_ref) | copy-start | bytes 3145732
  68.7 57.1 %copy-start.1 = (bf16[256,2048]{1,0:T(8,128)(2,1)S(1)}, bf16[256,2048]{1,0:T(8,128)(2,1)}, u32[]{:S(2)}) copy-start(bf16[256,2048]{1,0:T(8,128)(2,1)} %get-tuple-element.14.high_ref) | copy-start | bytes 3145732
  68.7 57.1 %copy-start.2 = (bf16[256,2048]{1,0:T(8,128)(2,1)S(1)}, bf16[256,2048]{1,0:T(8,128)(2,1)}, u32[]{:S(2)}) copy-start(bf16[256,2048]{1,0:T(8,128)(2,1)} %get-tuple-element.15.low_ref) | copy-start | bytes 3145732
  69.8 1.4 collective-permute-start.14
  72.2 4.2 %collective-permute-start.15 = (f32[8,640]{1,0:T(8,128)S(1)}, f32[8,640]{1,0:T(8,128)S(1)}, u32[]{:S(2)}, u32[]{:S(2)}) collective-permute-start(f32[8,640]{1,0:T(8,128)S(1)} %get-tuple-element.34), channel_id=1, source_target_pairs={{0,3},{1,2},{2,1},{3,0},{4,7},{5,6},{6,5},{7,4},{8,11},{9,10},{10,... | collective-permute-start | bytes 61448 | tf_op jit(solution)/shard_map/ppermute | solution.py:206
  72.3 5.6 %collective-permute-start.16 = (f32[8,640]{1,0:T(8,128)S(1)}, f32[8,640]{1,0:T(8,128)S(1)}, u32[]{:S(2)}, u32[]{:S(2)}) collective-permute-start(f32[8,640]{1,0:T(8,128)S(1)} %get-tuple-element.36), channel_id=1, source_target_pairs={{0,5},{1,4},{2,7},{3,6},{4,1},{5,0},{6,3},{7,2},{8,13},{9,12},{10,... | collective-permute-start | bytes 61448 | tf_op jit(solution)/shard_map/ppermute | solution.py:206
  76.2 3.8 %collective-permute-start.17 = (f32[8,640]{1,0:T(8,128)S(1)}, f32[8,640]{1,0:T(8,128)S(1)}, u32[]{:S(2)}, u32[]{:S(2)}) collective-permute-start(f32[8,640]{1,0:T(8,128)S(1)} %get-tuple-element.35), channel_id=1, source_target_pairs={{0,6},{1,7},{2,4},{3,5},{4,2},{5,3},{6,0},{7,1},{8,14},{9,15},{10,... | collective-permute-start | bytes 61448 | tf_op jit(solution)/shard_map/ppermute | solution.py:206
  80.1 5.2 %collective-permute-start.18 = (f32[8,640]{1,0:T(8,128)S(1)}, f32[8,640]{1,0:T(8,128)S(1)}, u32[]{:S(2)}, u32[]{:S(2)}) collective-permute-start(f32[8,640]{1,0:T(8,128)S(1)} %add_add_fusion.1), channel_id=1, source_target_pairs={{0,65},{1,64},{64,1},{65,0},{128,193},{129,192},{192,129},{193,128... | collective-permute-start | bytes 61448 | tf_op jit(solution)/shard_map/ppermute | solution.py:206
  82.8 4.7 %collective-permute-start.19 = (f32[8,640]{1,0:T(8,128)S(1)}, f32[8,640]{1,0:T(8,128)S(1)}, u32[]{:S(2)}, u32[]{:S(2)}) collective-permute-start(f32[8,640]{1,0:T(8,128)S(1)} %add_add_fusion.1), channel_id=1, source_target_pairs={{0,129},{1,128},{64,193},{65,192},{128,1},{129,0},{192,65},{193,64... | collective-permute-start | bytes 61448 | tf_op jit(solution)/shard_map/ppermute | solution.py:206
  84.4 3.8 %collective-permute-start.20 = (f32[8,640]{1,0:T(8,128)S(1)}, f32[8,640]{1,0:T(8,128)S(1)}, u32[]{:S(2)}, u32[]{:S(2)}) collective-permute-start(f32[8,640]{1,0:T(8,128)S(1)} %add_add_fusion.1), channel_id=1, source_target_pairs={{0,192},{1,193},{64,128},{65,129},{128,64},{129,65},{192,0},{193,1... | collective-permute-start | bytes 61448 | tf_op jit(solution)/shard_map/ppermute | solution.py:206
  88.2 5.4 %collective-permute-start.21 = (f32[8,640]{1,0:T(8,128)S(1)}, f32[8,640]{1,0:T(8,128)S(1)}, u32[]{:S(2)}, u32[]{:S(2)}) collective-permute-start(f32[8,640]{1,0:T(8,128)S(1)} %add_add_fusion), channel_id=1, source_target_pairs={{0,9},{1,8},{8,1},{9,0},{16,25},{17,24},{24,17},{25,16},{32,41},{3... | collective-permute-start | bytes 61448 | tf_op jit(solution)/shard_map/ppermute | solution.py:188
  93.7 4.6 %collective-permute-start.22 = (f32[8,640]{1,0:T(8,128)S(1)}, f32[8,640]{1,0:T(8,128)S(1)}, u32[]{:S(2)}, u32[]{:S(2)}) collective-permute-start(f32[8,640]{1,0:T(8,128)S(1)} %add.153), channel_id=1, source_target_pairs={{0,17},{1,16},{8,25},{9,24},{16,1},{17,0},{24,9},{25,8},{32,49},{3... | collective-permute-start | bytes 61448 | tf_op jit(solution)/shard_map/ppermute | solution.py:188
  98.2 7.1 %collective-permute-start.23 = (f32[8,640]{1,0:T(8,128)S(1)}, f32[8,640]{1,0:T(8,128)S(1)}, u32[]{:S(2)}, u32[]{:S(2)}) collective-permute-start(f32[8,640]{1,0:T(8,128)S(1)} %add.154), channel_id=1, source_target_pairs={{0,49},{1,48},{8,57},{9,56},{16,33},{17,32},{24,41},{25,40},{32,17... | collective-permute-start | bytes 61448 | tf_op jit(solution)/shard_map/ppermute | solution.py:188
  105.4 3.8 %collective-permute-start.26 = (f32[8,640]{1,0:T(8,128)S(1)}, f32[8,640]{1,0:T(8,128)S(1)}, u32[]{:S(2)}, u32[]{:S(2)}) collective-permute-start(f32[8,640]{1,0:T(8,128)S(1)} %add.155), channel_id=1, source_target_pairs={{0,3},{1,2},{2,1},{3,0},{4,7},{5,6},{6,5},{7,4},{8,11},{9,10},{10,... | collective-permute-start | bytes 61448 | tf_op jit(solution)/shard_map/ppermute | solution.py:206
  105.4 4.4 %collective-permute-start.24 = (f32[8,640]{1,0:T(8,128)S(1)}, f32[8,640]{1,0:T(8,128)S(1)}, u32[]{:S(2)}, u32[]{:S(2)}) collective-permute-start(f32[8,640]{1,0:T(8,128)S(1)} %add.155), channel_id=1, source_target_pairs={{0,6},{1,7},{2,4},{3,5},{4,2},{5,3},{6,0},{7,1},{8,14},{9,15},{10,... | collective-permute-start | bytes 61448 | tf_op jit(solution)/shard_map/ppermute | solution.py:206
  105.7 5.0 %collective-permute-start.25 = (f32[8,640]{1,0:T(8,128)S(1)}, f32[8,640]{1,0:T(8,128)S(1)}, u32[]{:S(2)}, u32[]{:S(2)}) collective-permute-start(f32[8,640]{1,0:T(8,128)S(1)} %add.155), channel_id=1, source_target_pairs={{0,5},{1,4},{2,7},{3,6},{4,1},{5,0},{6,3},{7,2},{8,13},{9,12},{10,... | collective-permute-start | bytes 61448 | tf_op jit(solution)/shard_map/ppermute | solution.py:206
  110.7 1.4 collective-permute-start.27
  112.1 53.8 %copy-start = (f32[32,32768]{1,0:T(8,128)S(1)}, f32[32,32768]{1,0:T(8,128)}, u32[]{:S(2)}) copy-start(f32[32,32768]{1,0:T(8,128)} %refs_6_.5) | copy-start | bytes 12582916
  123.4 4.7 %collective-permute-start.41 = (f32[64,2048]{1,0:T(8,128)S(1)}, f32[64,2048]{1,0:T(8,128)S(1)}, u32[]{:S(2)}, u32[]{:S(2)}) collective-permute-start(f32[64,2048]{1,0:T(8,128)S(1)} %image.3.refs_2_), channel_id=1, source_target_pairs={{0,1},{1,0},{2,3},{3,2},{4,5},{5,4},{6,7},{7,6},{8,9},{9,8},{10,11... | collective-permute-start | bytes 1572872 | tf_op jit(solution)/shard_map/ppermute | solution.py:286
  123.6 13.1 %collective-permute-start.30 = (f32[64,2048]{1,0:T(8,128)S(1)}, f32[64,2048]{1,0:T(8,128)S(1)}, u32[]{:S(2)}, u32[]{:S(2)}) collective-permute-start(f32[64,2048]{1,0:T(8,128)S(1)} %image.3.refs_2_), channel_id=1, source_target_pairs={{0,6},{2,0},{4,2},{6,4},{1,7},{3,1},{5,3},{7,5},{8,14},{10,8},{12,... | collective-permute-start | bytes 1572872 | tf_op jit(solution)/shard_map/ppermute | solution.py:282
  127.1 11.7 %collective-permute-start.40 = (f32[64,2048]{1,0:T(8,128)S(1)}, f32[64,2048]{1,0:T(8,128)S(1)}, u32[]{:S(2)}, u32[]{:S(2)}) collective-permute-start(f32[64,2048]{1,0:T(8,128)S(1)} %image.2.refs_1_), channel_id=1, source_target_pairs={{0,1},{1,0},{2,3},{3,2},{4,5},{5,4},{6,7},{7,6},{8,9},{9,8},{10,11... | collective-permute-start | bytes 1572872 | tf_op jit(solution)/shard_map/ppermute | solution.py:286
  127.8 14.6 %collective-permute-start.28 = (f32[64,2048]{1,0:T(8,128)S(1)}, f32[64,2048]{1,0:T(8,128)S(1)}, u32[]{:S(2)}, u32[]{:S(2)}) collective-permute-start(f32[64,2048]{1,0:T(8,128)S(1)} %image.2.refs_1_), channel_id=1, source_target_pairs={{0,2},{2,4},{4,6},{6,0},{1,3},{3,5},{5,7},{7,1},{8,10},{10,12},{12... | collective-permute-start | bytes 1572872 | tf_op jit(solution)/shard_map/ppermute | solution.py:282
  127.9 25.8 %collective-permute-start.34 = (f32[64,2048]{1,0:T(8,128)S(1)}, f32[64,2048]{1,0:T(8,128)S(1)}, u32[]{:S(2)}, u32[]{:S(2)}) collective-permute-start(f32[64,2048]{1,0:T(8,128)S(1)} %image.3.refs_2_), channel_id=1, source_target_pairs={{0,2},{2,4},{4,6},{6,0},{1,3},{3,5},{5,7},{7,1},{8,10},{10,12},{12... | collective-permute-start | bytes 1572872 | tf_op jit(solution)/shard_map/ppermute | solution.py:282
  128.1 27.1 %collective-permute-start.35 = (f32[64,2048]{1,0:T(8,128)S(1)}, f32[64,2048]{1,0:T(8,128)S(1)}, u32[]{:S(2)}, u32[]{:S(2)}) collective-permute-start(f32[64,2048]{1,0:T(8,128)S(1)} %image.2.refs_1_), channel_id=1, source_target_pairs={{0,6},{2,0},{4,2},{6,4},{1,7},{3,1},{5,3},{7,5},{8,14},{10,8},{12,... | collective-permute-start | bytes 1572872 | tf_op jit(solution)/shard_map/ppermute | solution.py:282
  136.8 18.4 %collective-permute-start.39 = (f32[64,2048]{1,0:T(8,128)S(1)}, f32[64,2048]{1,0:T(8,128)S(1)}, u32[]{:S(2)}, u32[]{:S(2)}) collective-permute-start(f32[64,2048]{1,0:T(8,128)S(1)} %collective-permute-done.30.refs_2_), channel_id=1, source_target_pairs={{0,1},{1,0},{2,3},{3,2},{4,5},{5,4},{6,7},{7,6},{8,9},{9,8},{10,11... | collective-permute-start | bytes 1572872 | tf_op jit(solution)/shard_map/ppermute | solution.py:286
  138.8 20.4 %collective-permute-start.31 = (f32[64,2048]{1,0:T(8,128)S(1)}, f32[64,2048]{1,0:T(8,128)S(1)}, u32[]{:S(2)}, u32[]{:S(2)}) collective-permute-start(f32[64,2048]{1,0:T(8,128)S(1)} %collective-permute-done.30.refs_2_), channel_id=1, source_target_pairs={{0,6},{2,0},{4,2},{6,4},{1,7},{3,1},{5,3},{7,5},{8,14},{10,8},{12,... | collective-permute-start | bytes 1572872 | tf_op jit(solution)/shard_map/ppermute | solution.py:282
  142.5 22.5 %collective-permute-start.29 = (f32[64,2048]{1,0:T(8,128)S(1)}, f32[64,2048]{1,0:T(8,128)S(1)}, u32[]{:S(2)}, u32[]{:S(2)}) collective-permute-start(f32[64,2048]{1,0:T(8,128)S(1)} %collective-permute-done.28.refs_1_), channel_id=1, source_target_pairs={{0,2},{2,4},{4,6},{6,0},{1,3},{3,5},{5,7},{7,1},{8,10},{10,12},{12... | collective-permute-start | bytes 1572872 | tf_op jit(solution)/shard_map/ppermute | solution.py:282
  153.7 14.8 %collective-permute-start.38 = (f32[64,2048]{1,0:T(8,128)S(1)}, f32[64,2048]{1,0:T(8,128)S(1)}, u32[]{:S(2)}, u32[]{:S(2)}) collective-permute-start(f32[64,2048]{1,0:T(8,128)S(1)} %collective-permute-done.28.refs_1_), channel_id=1, source_target_pairs={{0,1},{1,0},{2,3},{3,2},{4,5},{5,4},{6,7},{7,6},{8,9},{9,8},{10,11... | collective-permute-start | bytes 1572872 | tf_op jit(solution)/shard_map/ppermute | solution.py:286
  155.2 15.8 %collective-permute-start.36 = (f32[64,2048]{1,0:T(8,128)S(1)}, f32[64,2048]{1,0:T(8,128)S(1)}, u32[]{:S(2)}, u32[]{:S(2)}) collective-permute-start(f32[64,2048]{1,0:T(8,128)S(1)} %collective-permute-done.34.refs_1_), channel_id=1, source_target_pairs={{0,1},{1,0},{2,3},{3,2},{4,5},{5,4},{6,7},{7,6},{8,9},{9,8},{10,11... | collective-permute-start | bytes 1572872 | tf_op jit(solution)/shard_map/ppermute | solution.py:286
  155.2 15.8 %collective-permute-start.37 = (f32[64,2048]{1,0:T(8,128)S(1)}, f32[64,2048]{1,0:T(8,128)S(1)}, u32[]{:S(2)}, u32[]{:S(2)}) collective-permute-start(f32[64,2048]{1,0:T(8,128)S(1)} %collective-permute-done.35.refs_2_), channel_id=1, source_target_pairs={{0,1},{1,0},{2,3},{3,2},{4,5},{5,4},{6,7},{7,6},{8,9},{9,8},{10,11... | collective-permute-start | bytes 1572872 | tf_op jit(solution)/shard_map/ppermute | solution.py:286
  159.2 14.4 %collective-permute-start.33 = (f32[64,2048]{1,0:T(8,128)S(1)}, f32[64,2048]{1,0:T(8,128)S(1)}, u32[]{:S(2)}, u32[]{:S(2)}) collective-permute-start(f32[64,2048]{1,0:T(8,128)S(1)} %collective-permute-done.31.refs_2_), channel_id=1, source_target_pairs={{0,1},{1,0},{2,3},{3,2},{4,5},{5,4},{6,7},{7,6},{8,9},{9,8},{10,11... | collective-permute-start | bytes 1572872 | tf_op jit(solution)/shard_map/ppermute | solution.py:286
  164.9 8.7 %collective-permute-start.32 = (f32[64,2048]{1,0:T(8,128)S(1)}, f32[64,2048]{1,0:T(8,128)S(1)}, u32[]{:S(2)}, u32[]{:S(2)}) collective-permute-start(f32[64,2048]{1,0:T(8,128)S(1)} %collective-permute-done.29.refs_1_), channel_id=1, source_target_pairs={{0,1},{1,0},{2,3},{3,2},{4,5},{5,4},{6,7},{7,6},{8,9},{9,8},{10,11... | collective-permute-start | bytes 1572872 | tf_op jit(solution)/shard_map/ppermute | solution.py:286
  (15 other events, 152.2 us)

commit v3 on v2

--- a/solution.py
+++ b/solution.py
@@ -17,6 +17,8 @@
 FRM = ("y", "core")
 VOX = ("x", "z")
 MEMBERS = SIZES["y"] * SIZES["core"]
+CHUNK = 512
+PARTS = (3072, 1024)
 NT = (((1,), (1,)), ((), ()))
 PAIRS = [(i, j) for i in range(FRAMES // BLOCK) for j in range(i, FRAMES // BLOCK)]
 
@@ -29,76 +31,83 @@
 
 def gram_kernel(place_ref, *refs):
     pieces, before_ref = refs[:MEMBERS], refs[MEMBERS]
-    packed_ref, high_ref, low_ref, main, cross = refs[MEMBERS + 1 :]
-    step, rows = pl.program_id(0), pieces[0].shape[0]
-
-    @pl.when(step == 0)
-    def _():
-        main[...] = jnp.zeros_like(main)
-        cross[...] = jnp.zeros_like(cross)
-
-    for mask, piece_ref in enumerate(pieces):
-        mine = pl.ds(pl.multiple_of((place_ref[0] ^ mask) * rows, rows), rows)
-        high_ref[mine, :], low_ref[mine, :] = split(piece_ref[...])
-    high, low = high_ref[...], low_ref[...]
-    main[...] += lax.dot_general(high, high, NT, preferred_element_type=jnp.float32)
-    cross[...] += lax.dot_general(high, low, NT, preferred_element_type=jnp.float32)
-
-    @pl.when(step == pl.num_programs(0) - 1)
-    def _():
-        total = main[...] + cross[...] + cross[...].T
-        packed_ref[...] = before_ref[...] + jnp.concatenate(
-            [total[i * BLOCK : (i + 1) * BLOCK, j * BLOCK : (j + 1) * BLOCK] for i, j in PAIRS], axis=1
-        )
+    packed_ref, high_out, low_out, columns, high, low, main, cross, in_sems, out_sems = refs[MEMBERS + 1 :]
+    rows, width = pieces[0].shape
+    count = width // CHUNK
+
+    def part(n):
+        return pl.ds(pl.multiple_of(n * CHUNK, CHUNK), CHUNK)
+
+    def arrivals(n):
+        return [
+            pltpu.make_async_copy(
+                piece_ref.at[:, part(n)],
+                columns.at[pl.ds(pl.multiple_of((place_ref[0] ^ mask) * rows, rows), rows), part(n)],
+                in_sems.at[n, mask],
+            )
+            for mask, piece_ref in enumerate(pieces)
+        ]
+
+    def departures(n):
+        return [
+            pltpu.make_async_copy(source.at[:, part(n)], target.at[:, part(n)], out_sems.at[n, at])
+            for at, (source, target) in enumerate(((high, high_out), (low, low_out)))
+        ]
+
+    for n in range(count):
+        for copy in arrivals(n):
+            copy.start()
+    for n in range(count):
+        for copy in arrivals(n):
+            copy.wait()
+        first, second = split(columns[:, part(n)])
+        high[:, part(n)], low[:, part(n)] = first, second
+        product = lax.dot_general(first, first, NT, preferred_element_type=jnp.float32)
+        mixed = lax.dot_general(first, second, NT, preferred_element_type=jnp.float32)
+        main[...] = product if n == 0 else main[...] + product
+        cross[...] = mixed if n == 0 else cross[...] + mixed
+        for copy in departures(n):
+            copy.start()
+    total = main[...] + cross[...] + cross[...].T
+    packed_ref[...] = before_ref[...] + jnp.concatenate(
+        [total[i * BLOCK : (i + 1) * BLOCK, j * BLOCK : (j + 1) * BLOCK] for i, j in PAIRS], axis=1
+    )
+    for n in range(count):
+        for copy in departures(n):
+            copy.wait()
+
+
+def in_hbm(value):
+    return pltpu.with_memory_space_constraint(value, pltpu.HBM)
 
 
 def gram_packed(place, pieces, before):
-    chunk = 512
-    rows, width = pieces[0].shape
-    packed = pl.BlockSpec((BLOCK, BLOCK * len(PAIRS)), lambda n, place: (0, 0))
-    parts = pl.BlockSpec((FRAMES, chunk), lambda n, place: (0, n))
+    _, width = pieces[0].shape
+    vmem, hbm = pl.BlockSpec(memory_space=pltpu.VMEM), pl.BlockSpec(memory_space=pltpu.HBM)
     return pl.pallas_call(
         gram_kernel,
         out_shape=(
             jax.ShapeDtypeStruct(before.shape, jnp.float32),
-            jax.ShapeDtypeStruct((FRAMES, width), jnp.bfloat16),
-            jax.ShapeDtypeStruct((FRAMES, width), jnp.bfloat16),
-        ),
-        grid_spec=pltpu.PrefetchScalarGridSpec(
-            num_scalar_prefetch=1,
-            grid=(width // chunk,),
-            in_specs=[pl.BlockSpec((rows, chunk), lambda n, place: (0, n))] * MEMBERS + [packed],
-            out_specs=(packed, parts, parts),
-            scratch_shapes=[pltpu.VMEM((FRAMES, FRAMES), jnp.float32)] * 2,
-        ),
-        compiler_params=pltpu.CompilerParams(vmem_limit_bytes=60 << 20),
+            pltpu.HBM((FRAMES, width), jnp.bfloat16),
+            pltpu.HBM((FRAMES, width), jnp.bfloat16),
+        ),
+        in_specs=[pl.BlockSpec(memory_space=pltpu.SMEM)] + [hbm] * MEMBERS + [vmem],
+        out_specs=(vmem, hbm, hbm),
+        scratch_shapes=[
+            pltpu.VMEM((FRAMES, width), jnp.float32),
+            pltpu.VMEM((FRAMES, width), jnp.bfloat16),
+            pltpu.VMEM((FRAMES, width), jnp.bfloat16),
+            pltpu.VMEM((FRAMES, FRAMES), jnp.float32),
+            pltpu.VMEM((FRAMES, FRAMES), jnp.float32),
+            pltpu.SemaphoreType.DMA((width // CHUNK, MEMBERS)),
+            pltpu.SemaphoreType.DMA((width // CHUNK, 2)),
+        ],
+        compiler_params=pltpu.CompilerParams(vmem_limit_bytes=16 << 20),
         cost_estimate=pl.CostEstimate(
             flops=2 * 3 * FRAMES * FRAMES * width, bytes_accessed=4 << 20, transcendentals=0
         ),
         name="gram",
     )(place, *pieces, before)
-
-
-def image_kernel(turned_ref, high_ref, low_ref, image_ref):
-    high, low = split(turned_ref[...])
-    dot = functools.partial(jnp.dot, preferred_element_type=jnp.float32)
-    image_ref[...] = dot(high, high_ref[...]) + (dot(high, low_ref[...]) + dot(low, high_ref[...]))
-
-
-def image_of(turned, high, low):
-    chunk = 512
-    width = high.shape[1]
-    parts = pl.BlockSpec((FRAMES, chunk), lambda n: (0, n))
-    return pl.pallas_call(
-        image_kernel,
-        out_shape=jax.ShapeDtypeStruct((VECS, width), jnp.float32),
-        grid=(width // chunk,),
-        in_specs=[pl.BlockSpec((VECS, FRAMES), lambda n: (0, 0)), parts, parts],
-        out_specs=pl.BlockSpec((VECS, chunk), lambda n: (0, n)),
-        compiler_params=pltpu.CompilerParams(vmem_limit_bytes=8 << 20),
-        cost_estimate=pl.CostEstimate(flops=2 * 3 * VECS * FRAMES * width, bytes_accessed=4 << 20, transcendentals=0),
-        name="image",
-    )(turned, high, low)
 
 
 def inverse_factor(small):
@@ -144,7 +153,22 @@
     return jnp.concatenate(scaled, axis=0)[:, size:]
 
 
-def iterate_kernel(place_ref, packed_ref, start_ref, turned_ref, mine_ref, gram, vectors):
+def iterate_kernel(place_ref, packed_ref, start_ref, *refs):
+    parts = (len(refs) - 9) // 2
+    sources, refs = refs[: 2 * parts], refs[2 * parts :]
+    turned_ref, mine_ref, left_ref, right_ref, gram, vectors, high, low, sems = refs
+    copies, offset = [], 0
+    for n in range(parts):
+        width = sources[2 * n].shape[1]
+        for at, target in enumerate((high, low)):
+            copies.append(
+                pltpu.make_async_copy(
+                    sources[2 * n + at], target.at[:, offset : offset + width], sems.at[n, at]
+                )
+            )
+        offset += width
+    for copy in copies:
+        copy.start()
     for n, (i, j) in enumerate(PAIRS):
         block = packed_ref[:, n * BLOCK : (n + 1) * BLOCK]
         gram[i * BLOCK : (i + 1) * BLOCK, j * BLOCK : (j + 1) * BLOCK] = block
@@ -161,26 +185,45 @@
         small = dot(projected, projected, NT)
         turned_ref[...] = dot(inverse_factor(small), projected, (((1,), (0,)), ((), ())))
 
-    vectors[...] = turned_ref[...].T
+    turned = turned_ref[...]
+    vectors[...] = turned.T
     rows = mine_ref.shape[0]
     mine_ref[...] = vectors[pl.ds(pl.multiple_of(place_ref[0] * rows, rows), rows), :]
-
-
-def iterate(place, packed, turned, rows):
-    vmem = pl.BlockSpec(memory_space=pltpu.VMEM)
+    for copy in copies:
+        copy.wait()
+    first, second = split(turned)
+    for n, image_ref in enumerate((left_ref, right_ref)):
+        width = image_ref.shape[1]
+        some, rest = high[:, n * width : (n + 1) * width], low[:, n * width : (n + 1) * width]
+        dot = functools.partial(jnp.dot, preferred_element_type=jnp.float32)
+        image_ref[...] = dot(first, some) + (dot(first, rest) + dot(second, some))
+
+
+def iterate(place, packed, turned, columns, rows):
+    vmem, hbm = pl.BlockSpec(memory_space=pltpu.VMEM), pl.BlockSpec(memory_space=pltpu.HBM)
+    width = sum(high.shape[1] for high, _ in columns)
+    image = jax.ShapeDtypeStruct((VECS, width // 2), jnp.float32)
     return pl.pallas_call(
         iterate_kernel,
         out_shape=(
             jax.ShapeDtypeStruct((VECS, FRAMES), jnp.float32),
             jax.ShapeDtypeStruct((rows, VECS), jnp.float32),
-        ),
-        in_specs=[pl.BlockSpec(memory_space=pltpu.SMEM), vmem, vmem],
-        out_specs=(vmem, vmem),
-        scratch_shapes=[pltpu.VMEM((FRAMES, FRAMES), jnp.float32), pltpu.VMEM((FRAMES, VECS), jnp.float32)],
-        compiler_params=pltpu.CompilerParams(vmem_limit_bytes=8 << 20),
+            image,
+            image,
+        ),
+        in_specs=[pl.BlockSpec(memory_space=pltpu.SMEM), vmem, vmem] + [hbm] * 2 * len(columns),
+        out_specs=(vmem,) * 4,
+        scratch_shapes=[
+            pltpu.VMEM((FRAMES, FRAMES), jnp.float32),
+            pltpu.VMEM((FRAMES, VECS), jnp.float32),
+            pltpu.VMEM((FRAMES, width), jnp.bfloat16),
+            pltpu.VMEM((FRAMES, width), jnp.bfloat16),
+            pltpu.SemaphoreType.DMA((len(columns), 2)),
+        ],
+        compiler_params=pltpu.CompilerParams(vmem_limit_bytes=16 << 20),
         cost_estimate=pl.CostEstimate(flops=1 << 30, bytes_accessed=1 << 20, transcendentals=0),
         name="iterate",
-    )(place, packed, turned)
+    )(place, packed, turned, *[in_hbm(part) for pair in columns for part in pair])
 
 
 def exchange(value, axis, mask):
@@ -209,16 +252,15 @@
 
 def total_of(packed):
     x, z, y, core = (lax.axis_index(axis) for axis in SIZES)
-    lane = (core ^ x ^ (x >> 1) ^ z ^ (z >> 1) ^ y ^ (y >> 1)) & 1
+    lane = (core ^ x ^ z ^ (z >> 1) ^ y ^ (y >> 1)) & 1
     kept, sent = halves(packed, lane)
     value = kept + swap(sent)
     rows = value.shape[0] // 4
     parts = [lax.dynamic_slice_in_dim(value, (y ^ mask) * rows, rows, axis=0) for mask in range(4)]
-    for axis, values in (("y", parts), ("x", None)):
-        a, b, c, d = exchanges(values or [value] * 4, axis)
-        value = (a + b) + (c + d)
-    for mask in (1, 2, 6):
-        value = value + exchange(value, "z", mask)
+    a, b, c, d = exchanges(parts, "y")
+    value = (a + b) + (c + d)
+    for axis, mask in (("x", 1), ("x", 3), ("z", 1), ("z", 2), ("z", 6)):
+        value = value + exchange(value, axis, mask)
     a, b, c, d = exchanges([value] * 4, "y")
     odd, high = (y & 1) == 1, (y >> 1) == 1
     a, b, c, d = jnp.where(odd, b, a), jnp.where(odd, a, b), jnp.where(odd, d, c), jnp.where(odd, c, d)
@@ -289,33 +331,34 @@
 def body(casorati, start):
     index = lax.axis_index(FRM)
     place = index.reshape(1)
-    rows, width = casorati.shape[0], casorati.shape[1] // MEMBERS // 2
+    rows, block = casorati.shape[0], casorati.shape[1] // MEMBERS
     packed = jnp.zeros((BLOCK, BLOCK * len(PAIRS)), jnp.float32)
-    halved = []
-    gathered = []
-    for half in range(2):
-        pieces = []
-        for mask in range(MEMBERS):
-            piece = lax.dynamic_slice(casorati, (0, ((index ^ mask) * 2 + half) * width), (rows, width))
-            if mask:
-                piece = lax.ppermute(piece, FRM, [(i, i ^ mask) for i in range(MEMBERS)])
-            pieces.append(piece)
-        gathered.append(pieces)
-    for pieces in gathered:
-        packed, *parts = gram_packed(place, pieces, packed)
-        halved.append(parts)
-    turned, mine = iterate(place, total_of(packed), start.T, rows)
-    left, right = (image_of(turned, *parts) for parts in halved)
+    source, offset, slices, columns = casorati, 0, [], []
+    for width in PARTS:
+        slices.append(
+            [lax.dynamic_slice(source, (0, (index ^ mask) * block + offset), (rows, width)) for mask in range(MEMBERS)]
+        )
+        offset += width
+        source = lax.optimization_barrier((source, *slices[-1]))[0]
+    for pieces in slices:
+        for mask in range(1, MEMBERS):
+            pieces[mask] = lax.ppermute(pieces[mask], FRM, [(i, i ^ mask) for i in range(MEMBERS)])
+    for part, pieces in enumerate(slices):
+        packed, *found = gram_packed(place, pieces if part else [in_hbm(piece) for piece in pieces], packed)
+        columns.append(found)
+    turned, mine, left, right = iterate(place, total_of(packed), start.T, columns, rows)
 
     up_left, down_right = shift(left, 1), shift(right, -1)
     up_right, down_left = shift(right, 1), shift(left, -1)
-    far_left, far_right = shift(up_left, 1), shift(down_right, -1)
     groups = {
         "near": [(0, 0, left), (0, 1, right)],
         "first": [(-1, 0, up_left), (1, 1, down_right)],
         "second": [(-1, 1, up_right), (1, 0, down_left)],
-        "far": [(2, 0, far_left), (2, 1, far_right)],
     }
+    for part in range(2):
+        width = left.shape[1] // 2
+        far = [value[:, part * width : (part + 1) * width] for value in (up_left, down_right)]
+        groups[f"far{part}"] = [(2, part, shift(far[0], 1)), (2, 2 + part, shift(far[1], -1))]
     filtered = None
     for parts in groups.values():
         pieces = [(up, 0, side, value) for up, side, value in parts]

time: 177 us -> 172 us (0.972)
  Pallas kernels: 32.3 us -> 28.2 us
  waiting for transfers between devices: 70.1 us -> 72.5 us
  other arithmetic: 2.1 us -> 0.09 us
    ppermute x9 -> x6, starting transfers between devices: 13.2 us -> 8.05 us  [exchanges(): found.append(lax.ppermute(values[mask], (axis, 'core'), pairs))]
    ppermute x10 -> x12, starting transfers between devices: 7.43 us -> 11.8 us  [swap(): return lax.ppermute(value, 'core', [(0, 1), (1, 0)])]
    pallas_call x2, Pallas kernels: 10.2 us -> 6.07 us  [gram_packed(): pl.pallas_call(gram_kernel, out_shape=(jax.ShapeDtypeStruct(before.shape,...]
    ppermute x3 -> x5, waiting for transfers between devices: 4.4 us -> 8.11 us  [exchange(): return lax.ppermute(value, (axis, 'core'), pairs)]
    ppermute x3 -> x5, starting transfers between devices: 12.7 us -> 16 us  [exchange(): return lax.ppermute(value, (axis, 'core'), pairs)]
    ppermute x9 -> x6, waiting for transfers between devices: 8.12 us -> 5.29 us  [exchanges(): found.append(lax.ppermute(values[mask], (axis, 'core'), pairs))]
    ppermute x14, starting transfers between devices: 23.6 us -> 21 us  [body(): lax.ppermute(pieces[mask], FRM, [(i, i ^ mask) for i in range(MEMBERS)])]
    pallas_call x2 -> x0, Pallas kernels: 2.53 us -> none  [image_of(): pl.pallas_call(image_kernel, out_shape=jax.ShapeDtypeStruct((VECS, width)...]
  transfers between devices with their start and end apart: 42 -> 45, of which waited for: 22 -> 24; matrix products, arithmetic and copies ran while one was open for 0% -> 1% of each run, Pallas kernels for 8% -> 8%
where the time goes in v3:
time: 172 us
  waiting for transfers between devices  72.5 us (42%)
  starting transfers between devices  64.2 us (37%)
  Pallas kernels  28.2 us (16%)
  local copies, waits for them, and re-layouts  5.7 us (3%)
    ppermute x14, waiting for transfers between devices, body(): lax.ppermute(pieces[mask], FRM, [(i, i ^ mask) for i in range(MEMBERS)])  29.2 us
    ppermute x8, waiting for transfers between devices, shift(): lax.ppermute(value, 'y', [(i, (i + step) % SIZES['y']) for i in range(SIZ...  27.5 us
    ppermute x14, starting transfers between devices, body(): lax.ppermute(pieces[mask], FRM, [(i, i ^ mask) for i in range(MEMBERS)])  21 us
    ppermute x5, starting transfers between devices, exchange(): return lax.ppermute(value, (axis, 'core'), pairs)  16 us
    pallas_call x5, Pallas kernels, subtract(): pl.pallas_call(functools.partial(subtract_kernel, pieces), out_shape=jax....  12.3 us
    ppermute x12, starting transfers between devices, swap(): return lax.ppermute(value, 'core', [(0, 1), (1, 0)])  11.8 us
    pallas_call x1, Pallas kernels, iterate(): pl.pallas_call(iterate_kernel, out_shape=(jax.ShapeDtypeStruct((VECS, FRA...  9.89 us
    ppermute x5, waiting for transfers between devices, exchange(): return lax.ppermute(value, (axis, 'core'), pairs)  8.11 us
  transfers between devices with their start and end apart: 45, of which 24 were waited for; matrix products, arithmetic and copies ran while one was open for 1% of the time, Pallas kernels for 8%

profile of v3, /device:TPU:1, one launch (start us, length us, event | category | flops | bytes accessed | tf_op | source)
XLA Modules:
  0.0 171.6 jit_solution(9747365430856990058)
XLA Ops:
  0.7 2.8 %constant_dynamic-slice_fusion.11 = (f32[32,3072]{1,0:T(8,128)S(1)}, f32[32,3072]{1,0:T(8,128)S(1)}, f32[32,3072]{1,0:T(8,128)S(1)}, f32[32,3072]{1,0:T(8,128)S(...) fusion(f32[32,32768]{1,0:T(8,128)} %refs_6_.7, ...), kind=kLoop, calls=%fused_computation.20 | loop fusion | bytes 6291488 | tf_op jit(solution)/shard_map/dynamic_slice | solution.py:339
  3.5 3.7 %collective-permute-start.10 = (f32[32,3072]{1,0:T(8,128)S(1)}, f32[32,3072]{1,0:T(8,128)}, u32[]{:S(2)}, u32[]{:S(2)}) collective-permute-start(f32[32,3072]{1,0:T(8,128)S(1)} %get-tuple-element.35), channel_id=1, source_target_pairs={{0,4},{1,5},{2,6},{3,7},{4,0},{5,1},{6,2},{7,3},{8,12},{9,13},{10,... | collective-permute-start | bytes 1179656 | tf_op jit(solution)/shard_map/ppermute | solution.py:345
  7.2 2.6 %collective-permute-start.11 = (f32[32,3072]{1,0:T(8,128)S(1)}, f32[32,3072]{1,0:T(8,128)}, u32[]{:S(2)}, u32[]{:S(2)}) collective-permute-start(f32[32,3072]{1,0:T(8,128)S(1)} %get-tuple-element.34), channel_id=1, source_target_pairs={{0,5},{1,4},{2,7},{3,6},{4,1},{5,0},{6,3},{7,2},{8,13},{9,12},{10,... | collective-permute-start | bytes 1179656 | tf_op jit(solution)/shard_map/ppermute | solution.py:345
  9.9 2.1 %constant_dynamic-slice_fusion.3 = (f32[32,1024]{1,0:T(8,128)S(1)}, f32[32,1024]{1,0:T(8,128)}, f32[32,1024]{1,0:T(8,128)}, f32[32,1024]{1,0:T(8,128)}, f32[32,1...) fusion(f32[32,32768]{1,0:T(8,128)} %refs_6_.7, s32[]{:T(128)S(6)} %select_n.125, ...), kind=kLoop, calls=%fused_computation.12 | loop fusion | bytes 2097184 | tf_op jit(solution)/shard_map/dynamic_slice | solution.py:339
  12.1 1.5 collective-permute-start.12
  13.6 1.8 %collective-permute-start.13 = (f32[32,3072]{1,0:T(8,128)S(1)}, f32[32,3072]{1,0:T(8,128)S(1)}, u32[]{:S(2)}, u32[]{:S(2)}) collective-permute-start(f32[32,3072]{1,0:T(8,128)S(1)} %get-tuple-element.32), channel_id=1, source_target_pairs={{0,7},{1,6},{2,5},{3,4},{4,3},{5,2},{6,1},{7,0},{8,15},{9,14},{10,... | collective-permute-start | bytes 1179656 | tf_op jit(solution)/shard_map/ppermute | solution.py:345
  15.4 12.1 %collective-permute-done.1.refs_2_ = f32[32,1024]{1,0:T(8,128)S(1)} collective-permute-done((f32[32,1024]{1,0:T(8,128)S(1)}, f32[32,1024]{1,0:T(8,128)S(1)}, u32[]{:S(2)}, u32[]{:S(2)}) %collective-permute-start.1) | collective-permute-done | bytes 131104 | tf_op jit(solution)/shard_map/ppermute | solution.py:345
  27.5 1.5 collective-permute-start.7
  30.6 3.1 %collective-permute-done.12.refs_6_ = f32[32,3072]{1,0:T(8,128)S(1)} collective-permute-done((f32[32,3072]{1,0:T(8,128)S(1)}, f32[32,3072]{1,0:T(8,128)S(1)}, u32[]{:S(2)}, u32[]{:S(2)}) %collective-permute-start.12) | collective-permute-done | bytes 393248 | tf_op jit(solution)/shard_map/ppermute | solution.py:345
  33.7 1.8 %collective-permute-start.2 = (f32[32,1024]{1,0:T(8,128)}, f32[32,1024]{1,0:T(8,128)S(1)}, u32[]{:S(2)}, u32[]{:S(2)}) collective-permute-start(f32[32,1024]{1,0:T(8,128)} %get-tuple-element.28), channel_id=1, source_target_pairs={{0,3},{1,2},{2,1},{3,0},{4,7},{5,6},{6,5},{7,4},{8,11},{9,10},{10,... | collective-permute-start | bytes 393224 | tf_op jit(solution)/shard_map/ppermute | solution.py:345
  35.5 6.6 %collective-permute-done.13.refs_7_ = f32[32,3072]{1,0:T(8,128)S(1)} collective-permute-done((f32[32,3072]{1,0:T(8,128)S(1)}, f32[32,3072]{1,0:T(8,128)S(1)}, u32[]{:S(2)}, u32[]{:S(2)}) %collective-permute-start.13) | collective-permute-done | bytes 393248 | tf_op jit(solution)/shard_map/ppermute | solution.py:345
  42.1 3.0 %collective-permute-start.3 = (f32[32,1024]{1,0:T(8,128)}, f32[32,1024]{1,0:T(8,128)S(1)}, u32[]{:S(2)}, u32[]{:S(2)}) collective-permute-start(f32[32,1024]{1,0:T(8,128)} %get-tuple-element.27), channel_id=1, source_target_pairs={{0,4},{1,5},{2,6},{3,7},{4,0},{5,1},{6,2},{7,3},{8,12},{9,13},{10,... | collective-permute-start | bytes 393224 | tf_op jit(solution)/shard_map/ppermute | solution.py:345
  45.7 2.8 %collective-permute-start.5 = (f32[32,1024]{1,0:T(8,128)}, f32[32,1024]{1,0:T(8,128)S(1)}, u32[]{:S(2)}, u32[]{:S(2)}) collective-permute-start(f32[32,1024]{1,0:T(8,128)} %get-tuple-element.25), channel_id=1, source_target_pairs={{0,6},{1,7},{2,4},{3,5},{4,2},{5,3},{6,0},{7,1},{8,14},{9,15},{10,... | collective-permute-start | bytes 393224 | tf_op jit(solution)/shard_map/ppermute | solution.py:345
  49.8 4.3 %gram.2 = (f32[64,640]{1,0:T(8,128)S(1)}, bf16[256,3072]{1,0:T(8,128)(2,1)}, bf16[256,3072]{1,0:T(8,128)(2,1)}) custom-call(s32[1]{0:T(128)} %bitcast.place_ref, f32[32,3072]{1,0:T(8,128)} %get-tuple-element.39.refs_0_, f32[32,3072]{1,0:T(8,128)} %copy-done.4, f32[32,3072]{1,0:T(8,128)} %copy-done.5, f32[32,3072]{1,0:T(8,128)} %copy-done.6, ...), custom_call_target="tpu_custom_call" | custom-call | flops 1207959552 | bytes 4194304 | tf_op jit(solution)/shard_map/gram/pallas_call | solution.py:87
  54.1 2.8 %collective-permute-done.4.refs_5_ = f32[32,1024]{1,0:T(8,128)S(1)} collective-permute-done((f32[32,1024]{1,0:T(8,128)}, f32[32,1024]{1,0:T(8,128)S(1)}, u32[]{:S(2)}, u32[]{:S(2)}) %collective-permute-start.4) | collective-permute-done | bytes 131104 | tf_op jit(solution)/shard_map/ppermute | solution.py:345
  57.8 3.1 %collective-permute-done.6.refs_7_ = f32[32,1024]{1,0:T(8,128)S(1)} collective-permute-done((f32[32,1024]{1,0:T(8,128)S(1)}, f32[32,1024]{1,0:T(8,128)S(1)}, u32[]{:S(2)}, u32[]{:S(2)}) %collective-permute-start.6) | collective-permute-done | bytes 131104 | tf_op jit(solution)/shard_map/ppermute | solution.py:345
  60.8 1.8 %gram.3 = (f32[64,640]{1,0:T(8,128)S(1)}, bf16[256,1024]{1,0:T(8,128)(2,1)}, bf16[256,1024]{1,0:T(8,128)(2,1)}) custom-call(s32[1]{0:T(128)} %bitcast.place_ref, f32[32,1024]{1,0:T(8,128)S(1)} %get-tuple-element.31.refs_0_, f32[32,1024]{1,0:T(8,128)S(1)} %collective-permute-done.refs_1_, f32[32,1024]{1,0:T(8,128)S(1)} %collective-permute-done.1.refs_2_, ...), custom_call_target="tpu_custom_call" | custom-call | flops 402653184 | bytes 4194304 | tf_op jit(solution)/shard_map/gram/pallas_call | solution.py:87
  64.4 4.0 %collective-permute-start.16 = (f32[8,640]{1,0:T(8,128)S(1)}, f32[8,640]{1,0:T(8,128)S(1)}, u32[]{:S(2)}, u32[]{:S(2)}) collective-permute-start(f32[8,640]{1,0:T(8,128)S(1)} %get-tuple-element.46), channel_id=1, source_target_pairs={{0,5},{1,4},{2,7},{3,6},{4,1},{5,0},{6,3},{7,2},{8,13},{9,12},{10,... | collective-permute-start | bytes 61448 | tf_op jit(solution)/shard_map/ppermute | solution.py:249
  68.3 1.8 %collective-permute-done.16 = f32[8,640]{1,0:T(8,128)S(1)} collective-permute-done((f32[8,640]{1,0:T(8,128)S(1)}, f32[8,640]{1,0:T(8,128)S(1)}, u32[]{:S(2)}, u32[]{:S(2)}) %collective-permute-start.16) | collective-permute-done | bytes 20512 | tf_op jit(solution)/shard_map/ppermute | solution.py:249
  70.1 2.1 %collective-permute-done.17 = f32[8,640]{1,0:T(8,128)S(1)} collective-permute-done((f32[8,640]{1,0:T(8,128)S(1)}, f32[8,640]{1,0:T(8,128)S(1)}, u32[]{:S(2)}, u32[]{:S(2)}) %collective-permute-start.17) | collective-permute-done | bytes 20512 | tf_op jit(solution)/shard_map/ppermute | solution.py:249
  72.2 2.7 %collective-permute-start.18 = (f32[8,640]{1,0:T(8,128)S(1)}, f32[8,640]{1,0:T(8,128)S(1)}, u32[]{:S(2)}, u32[]{:S(2)}) collective-permute-start(f32[8,640]{1,0:T(8,128)S(1)} %add_add_fusion), channel_id=1, source_target_pairs={{0,65},{1,64},{64,1},{65,0},{128,193},{129,192},{192,129},{193,128... | collective-permute-start | bytes 61448 | tf_op jit(solution)/shard_map/ppermute | solution.py:231
  74.9 1.9 %collective-permute-done.18 = f32[8,640]{1,0:T(8,128)S(1)} collective-permute-done((f32[8,640]{1,0:T(8,128)S(1)}, f32[8,640]{1,0:T(8,128)S(1)}, u32[]{:S(2)}, u32[]{:S(2)}) %collective-permute-start.18) | collective-permute-done | bytes 20512 | tf_op jit(solution)/shard_map/ppermute | solution.py:231
  76.8 2.6 %collective-permute-start.19 = (f32[8,640]{1,0:T(8,128)S(1)}, f32[8,640]{1,0:T(8,128)S(1)}, u32[]{:S(2)}, u32[]{:S(2)}) collective-permute-start(f32[8,640]{1,0:T(8,128)S(1)} %add.163), channel_id=1, source_target_pairs={{0,193},{1,192},{64,129},{65,128},{128,65},{129,64},{192,1},{193,0... | collective-permute-start | bytes 61448 | tf_op jit(solution)/shard_map/ppermute | solution.py:231
  79.4 1.8 %collective-permute-done.19 = f32[8,640]{1,0:T(8,128)S(1)} collective-permute-done((f32[8,640]{1,0:T(8,128)S(1)}, f32[8,640]{1,0:T(8,128)S(1)}, u32[]{:S(2)}, u32[]{:S(2)}) %collective-permute-start.19) | collective-permute-done | bytes 20512 | tf_op jit(solution)/shard_map/ppermute | solution.py:231
  81.2 1.9 %collective-permute-start.20 = (f32[8,640]{1,0:T(8,128)S(1)}, f32[8,640]{1,0:T(8,128)S(1)}, u32[]{:S(2)}, u32[]{:S(2)}) collective-permute-start(f32[8,640]{1,0:T(8,128)S(1)} %add.164), channel_id=1, source_target_pairs={{0,9},{1,8},{8,1},{9,0},{16,25},{17,24},{24,17},{25,16},{32,41},{3... | collective-permute-start | bytes 61448 | tf_op jit(solution)/shard_map/ppermute | solution.py:231
  83.1 1.5 collective-permute-done.20
  84.6 3.1 %collective-permute-start.21 = (f32[8,640]{1,0:T(8,128)S(1)}, f32[8,640]{1,0:T(8,128)S(1)}, u32[]{:S(2)}, u32[]{:S(2)}) collective-permute-start(f32[8,640]{1,0:T(8,128)S(1)} %add.165), channel_id=1, source_target_pairs={{0,17},{1,16},{8,25},{9,24},{16,1},{17,0},{24,9},{25,8},{32,49},{3... | collective-permute-start | bytes 61448 | tf_op jit(solution)/shard_map/ppermute | solution.py:231
  87.7 1.5 collective-permute-done.21
  89.1 5.7 %collective-permute-start.22 = (f32[8,640]{1,0:T(8,128)S(1)}, f32[8,640]{1,0:T(8,128)S(1)}, u32[]{:S(2)}, u32[]{:S(2)}) collective-permute-start(f32[8,640]{1,0:T(8,128)S(1)} %add.166), channel_id=1, source_target_pairs={{0,49},{1,48},{8,57},{9,56},{16,33},{17,32},{24,41},{25,40},{32,17... | collective-permute-start | bytes 61448 | tf_op jit(solution)/shard_map/ppermute | solution.py:231
  94.9 1.5 collective-permute-done.22
  96.5 3.7 %collective-permute-start.24 = (f32[8,640]{1,0:T(8,128)S(1)}, f32[8,640]{1,0:T(8,128)S(1)}, u32[]{:S(2)}, u32[]{:S(2)}) collective-permute-start(f32[8,640]{1,0:T(8,128)S(1)} %add.167), channel_id=1, source_target_pairs={{0,5},{1,4},{2,7},{3,6},{4,1},{5,0},{6,3},{7,2},{8,13},{9,12},{10,... | collective-permute-start | bytes 61448 | tf_op jit(solution)/shard_map/ppermute | solution.py:249
  103.0 9.9 %iterate.1 = (f32[64,256]{1,0:T(8,128)}, f32[32,64]{1,0:T(8,128)S(1)}, f32[64,2048]{1,0:T(8,128)S(1)}, f32[64,2048]{1,0:T(8,128)S(1)}) custom-call(s32[1]{0:T(128)} %bitcast.place_ref, f32[64,640]{1,0:T(8,128)S(1)} %maximum_select_fusion.packed_ref, f32[64,256]{1,0:T(8,128)S(1)} %bitcast.3, bf16[256,3072]{1,0:T(8,128)(2,1)} %get-tuple-element.16.refs_0_, ...), custom_call_target="tpu_custom_call" | custom-call | flops 1073741824 | bytes 1048576 | tf_op jit(solution)/shard_map/iterate/pallas_call | solution.py:206
  114.0 1.7 %collective-permute-start.29 = (f32[64,2048]{1,0:T(8,128)S(1)}, f32[64,2048]{1,0:T(8,128)S(1)}, u32[]{:S(2)}, u32[]{:S(2)}) collective-permute-start(f32[64,2048]{1,0:T(8,128)S(1)} %get-tuple-element.23.refs_2_), channel_id=1, source_target_pairs={{0,6},{2,0},{4,2},{6,4},{1,7},{3,1},{5,3},{7,5},{8,14},{10,8},{12,... | collective-permute-start | bytes 1572872 | tf_op jit(solution)/shard_map/ppermute | solution.py:324
  116.5 11.0 %collective-permute-done.27.refs_1_ = f32[64,2048]{1,0:T(8,128)S(1)} collective-permute-done((f32[64,2048]{1,0:T(8,128)S(1)}, f32[64,2048]{1,0:T(8,128)S(1)}, u32[]{:S(2)}, u32[]{:S(2)}) %collective-permute-start.27) | collective-permute-done | bytes 524320 | tf_op jit(solution)/shard_map/ppermute | solution.py:324
  129.2 2.1 %collective-permute-start.34 = (f32[64,1024]{1,0:T(8,128)S(1)}, f32[64,1024]{1,0:T(8,128)S(1)}, u32[]{:S(2)}, u32[]{:S(2)}) collective-permute-start(f32[64,1024]{1,0:T(8,128)S(1)} %get-tuple-element.40), channel_id=1, source_target_pairs={{0,6},{2,0},{4,2},{6,4},{1,7},{3,1},{5,3},{7,5},{8,14},{10,8},{12,... | collective-permute-start | bytes 786440 | tf_op jit(solution)/shard_map/ppermute | solution.py:324
  131.3 7.5 %collective-permute-done.37.refs_1_ = f32[64,2048]{1,0:T(8,128)S(1)} collective-permute-done((f32[64,2048]{1,0:T(8,128)S(1)}, f32[64,2048]{1,0:T(8,128)S(1)}, u32[]{:S(2)}, u32[]{:S(2)}) %collective-permute-start.37) | collective-permute-done | bytes 524320 | tf_op jit(solution)/shard_map/ppermute | solution.py:324
  138.8 1.6 collective-permute-start.41
  140.4 3.6 %collective-permute-start.42 = (f32[64,2048]{1,0:T(8,128)S(1)}, f32[64,2048]{1,0:T(8,128)S(1)}, u32[]{:S(2)}, u32[]{:S(2)}) collective-permute-start(f32[64,2048]{1,0:T(8,128)S(1)} %collective-permute-done.29.refs_2_), channel_id=1, source_target_pairs={{0,1},{1,0},{2,3},{3,2},{4,5},{5,4},{6,7},{7,6},{8,9},{9,8},{10,11... | collective-permute-start | bytes 1572872 | tf_op jit(solution)/shard_map/ppermute | solution.py:328
  144.4 1.6 collective-permute-start.39
  146.0 1.5 collective-permute-start.40
  147.5 2.5 %collective-permute-done.28.refs_1_ = f32[64,1024]{1,0:T(8,128)S(1)} collective-permute-done((f32[64,1024]{1,0:T(8,128)S(1)}, f32[64,1024]{1,0:T(8,128)S(1)}, u32[]{:S(2)}, u32[]{:S(2)}) %collective-permute-start.28) | collective-permute-done | bytes 262176 | tf_op jit(solution)/shard_map/ppermute | solution.py:324
  150.9 6.0 %collective-permute-done.30.refs_2_ = f32[64,1024]{1,0:T(8,128)S(1)} collective-permute-done((f32[64,1024]{1,0:T(8,128)S(1)}, f32[64,1024]{1,0:T(8,128)S(1)}, u32[]{:S(2)}, u32[]{:S(2)}) %collective-permute-start.30) | collective-permute-done | bytes 262176 | tf_op jit(solution)/shard_map/ppermute | solution.py:324
  156.9 1.9 %collective-permute-start.35 = (f32[64,1024]{1,0:T(8,128)S(1)}, f32[64,1024]{1,0:T(8,128)S(1)}, u32[]{:S(2)}, u32[]{:S(2)}) collective-permute-start(f32[64,1024]{1,0:T(8,128)S(1)} %collective-permute-done.33.refs_1_), channel_id=1, source_target_pairs={{0,1},{1,0},{2,3},{3,2},{4,5},{5,4},{6,7},{7,6},{8,9},{9,8},{10,11... | collective-permute-start | bytes 786440 | tf_op jit(solution)/shard_map/ppermute | solution.py:328
  159.4 2.6 %subtract.5.refs_5_ = f32[32,32768]{1,0:T(8,128)} custom-call(s32[1]{0:T(128)} %bitcast.place_ref, f32[32,64]{1,0:T(8,128)S(1)} %get-tuple-element.21.refs_0_, f32[64,2048]{1,0:T(8,128)S(1)} %get-tuple-element.22.refs_1_, f32[64,2048]{1,0:T(8,128)S(1)} %get-tuple-element.23.refs_2_, f32[64,2048]{1,0:T(8,128)S(1)} %collective-permute-done.43.refs_3_, ...), custom_call_target="tpu_custom_call" | custom-call | flops 201326592 | bytes 4194304 | tf_op jit(solution)/shard_map/subtract/pallas_call | solution.py:308
  161.9 2.6 %subtract.6.refs_5_ = f32[32,32768]{1,0:T(8,128)} custom-call(s32[1]{0:T(128)} %bitcast.place_ref, f32[32,64]{1,0:T(8,128)S(1)} %get-tuple-element.21.refs_0_, f32[64,2048]{1,0:T(8,128)S(1)} %collective-permute-done.27.refs_1_, f32[64,2048]{1,0:T(8,128)S(1)} %collective-permute-done.29.refs_2_, ...), custom_call_target="tpu_custom_call", output_to_operand_aliasing={{}: (6, {})} | custom-call | flops 201326592 | bytes 4194304 | tf_op jit(solution)/shard_map/subtract/pallas_call | solution.py:308
  164.5 2.6 %subtract.7.refs_5_ = f32[32,32768]{1,0:T(8,128)} custom-call(s32[1]{0:T(128)} %bitcast.place_ref, f32[32,64]{1,0:T(8,128)S(1)} %get-tuple-element.21.refs_0_, f32[64,2048]{1,0:T(8,128)S(1)} %collective-permute-done.37.refs_1_, f32[64,2048]{1,0:T(8,128)S(1)} %collective-permute-done.38.refs_2_, ...), custom_call_target="tpu_custom_call", output_to_operand_aliasing={{}: (6, {})} | custom-call | flops 201326592 | bytes 4194304 | tf_op jit(solution)/shard_map/subtract/pallas_call | solution.py:308
  167.1 2.3 %subtract.8.refs_5_ = f32[32,32768]{1,0:T(8,128)} custom-call(s32[1]{0:T(128)} %bitcast.place_ref, f32[32,64]{1,0:T(8,128)S(1)} %get-tuple-element.21.refs_0_, f32[64,1024]{1,0:T(8,128)S(1)} %collective-permute-done.33.refs_1_, f32[64,1024]{1,0:T(8,128)S(1)} %collective-permute-done.34.refs_2_, ...), custom_call_target="tpu_custom_call", output_to_operand_aliasing={{}: (6, {})} | custom-call | flops 100663296 | bytes 4194304 | tf_op jit(solution)/shard_map/subtract/pallas_call | solution.py:308
  169.4 2.3 %subtract.9 = f32[32,32768]{1,0:T(8,128)} custom-call(s32[1]{0:T(128)} %bitcast.place_ref, f32[32,64]{1,0:T(8,128)S(1)} %get-tuple-element.21.refs_0_, f32[64,1024]{1,0:T(8,128)S(1)} %collective-permute-done.28.refs_1_, f32[64,1024]{1,0:T(8,128)S(1)} %collective-permute-done.30.refs_2_, ...), custom_call_target="tpu_custom_call", output_to_operand_aliasing={{}: (6, {})} | custom-call | flops 100663296 | bytes 4194304 | tf_op jit(solution)/shard_map/subtract/pallas_call | solution.py:308
  (82 shorter events, 14.5 us)
Async XLA Ops:
  3.5 25.5 %collective-permute-start.10 = (f32[32,3072]{1,0:T(8,128)S(1)}, f32[32,3072]{1,0:T(8,128)}, u32[]{:S(2)}, u32[]{:S(2)}) collective-permute-start(f32[32,3072]{1,0:T(8,128)S(1)} %get-tuple-element.35), channel_id=1, source_target_pairs={{0,4},{1,5},{2,6},{3,7},{4,0},{5,1},{6,2},{7,3},{8,12},{9,13},{10,... | collective-permute-start | bytes 1179656 | tf_op jit(solution)/shard_map/ppermute | solution.py:345
  7.2 22.8 %collective-permute-start.11 = (f32[32,3072]{1,0:T(8,128)S(1)}, f32[32,3072]{1,0:T(8,128)}, u32[]{:S(2)}, u32[]{:S(2)}) collective-permute-start(f32[32,3072]{1,0:T(8,128)S(1)} %get-tuple-element.34), channel_id=1, source_target_pairs={{0,5},{1,4},{2,7},{3,6},{4,1},{5,0},{6,3},{7,2},{8,13},{9,12},{10,... | collective-permute-start | bytes 1179656 | tf_op jit(solution)/shard_map/ppermute | solution.py:345
  12.0 91.0 %copy-start.1 = (f32[256,64]{0,1:T(8,128)S(1)}, f32[256,64]{0,1:T(8,128)}, u32[]{:S(2)}) copy-start(f32[256,64]{0,1:T(8,128)} %param.3) | copy-start | bytes 196612
  12.0 1.6 collective-permute-start
  12.0 15.5 %collective-permute-start.1 = (f32[32,1024]{1,0:T(8,128)S(1)}, f32[32,1024]{1,0:T(8,128)S(1)}, u32[]{:S(2)}, u32[]{:S(2)}) collective-permute-start(f32[32,1024]{1,0:T(8,128)S(1)} %get-tuple-element.29), channel_id=1, source_target_pairs={{0,2},{1,3},{2,0},{3,1},{4,6},{5,7},{6,4},{7,5},{8,10},{9,11},{10,... | collective-permute-start | bytes 393224 | tf_op jit(solution)/shard_map/ppermute | solution.py:345
  12.1 21.6 %collective-permute-start.12 = (f32[32,3072]{1,0:T(8,128)S(1)}, f32[32,3072]{1,0:T(8,128)S(1)}, u32[]{:S(2)}, u32[]{:S(2)}) collective-permute-start(f32[32,3072]{1,0:T(8,128)S(1)} %get-tuple-element.33), channel_id=1, source_target_pairs={{0,6},{1,7},{2,4},{3,5},{4,2},{5,3},{6,0},{7,1},{8,14},{9,15},{10,... | collective-permute-start | bytes 1179656 | tf_op jit(solution)/shard_map/ppermute | solution.py:345
  13.6 28.5 %collective-permute-start.13 = (f32[32,3072]{1,0:T(8,128)S(1)}, f32[32,3072]{1,0:T(8,128)S(1)}, u32[]{:S(2)}, u32[]{:S(2)}) collective-permute-start(f32[32,3072]{1,0:T(8,128)S(1)} %get-tuple-element.32), channel_id=1, source_target_pairs={{0,7},{1,6},{2,5},{3,4},{4,3},{5,2},{6,1},{7,0},{8,15},{9,14},{10,... | collective-permute-start | bytes 1179656 | tf_op jit(solution)/shard_map/ppermute | solution.py:345
  27.5 17.7 %collective-permute-start.7 = (f32[32,3072]{1,0:T(8,128)S(1)}, f32[32,3072]{1,0:T(8,128)S(1)}, u32[]{:S(2)}, u32[]{:S(2)}) collective-permute-start(f32[32,3072]{1,0:T(8,128)S(1)} %get-tuple-element.38), channel_id=1, source_target_pairs={{0,1},{1,0},{2,3},{3,2},{4,5},{5,4},{6,7},{7,6},{8,9},{9,8},{10,11... | collective-permute-start | bytes 1179656 | tf_op jit(solution)/shard_map/ppermute | solution.py:345
  29.0 16.7 %collective-permute-start.8 = (f32[32,3072]{1,0:T(8,128)S(1)}, f32[32,3072]{1,0:T(8,128)S(1)}, u32[]{:S(2)}, u32[]{:S(2)}) collective-permute-start(f32[32,3072]{1,0:T(8,128)S(1)} %get-tuple-element.37), channel_id=1, source_target_pairs={{0,2},{1,3},{2,0},{3,1},{4,6},{5,7},{6,4},{7,5},{8,10},{9,11},{10,... | collective-permute-start | bytes 1179656 | tf_op jit(solution)/shard_map/ppermute | solution.py:345
  30.1 19.0 %collective-permute-start.9 = (f32[32,3072]{1,0:T(8,128)S(1)}, f32[32,3072]{1,0:T(8,128)S(1)}, u32[]{:S(2)}, u32[]{:S(2)}) collective-permute-start(f32[32,3072]{1,0:T(8,128)S(1)} %get-tuple-element.36), channel_id=1, source_target_pairs={{0,3},{1,2},{2,1},{3,0},{4,7},{5,6},{6,5},{7,4},{8,11},{9,10},{10,... | collective-permute-start | bytes 1179656 | tf_op jit(solution)/shard_map/ppermute | solution.py:345
  33.7 15.3 %copy-start.2 = (f32[32,3072]{1,0:T(8,128)}, f32[32,3072]{1,0:T(8,128)S(1)}, u32[]{:S(2)}) copy-start(f32[32,3072]{1,0:T(8,128)S(1)} %collective-permute-done.12.refs_6_) | copy-start | bytes 1179652
  33.7 20.3 %collective-permute-start.2 = (f32[32,1024]{1,0:T(8,128)}, f32[32,1024]{1,0:T(8,128)S(1)}, u32[]{:S(2)}, u32[]{:S(2)}) collective-permute-start(f32[32,1024]{1,0:T(8,128)} %get-tuple-element.28), channel_id=1, source_target_pairs={{0,3},{1,2},{2,1},{3,0},{4,7},{5,6},{6,5},{7,4},{8,11},{9,10},{10,... | collective-permute-start | bytes 393224 | tf_op jit(solution)/shard_map/ppermute | solution.py:345
  42.1 12.0 %collective-permute-start.3 = (f32[32,1024]{1,0:T(8,128)}, f32[32,1024]{1,0:T(8,128)S(1)}, u32[]{:S(2)}, u32[]{:S(2)}) collective-permute-start(f32[32,1024]{1,0:T(8,128)} %get-tuple-element.27), channel_id=1, source_target_pairs={{0,4},{1,5},{2,6},{3,7},{4,0},{5,1},{6,2},{7,3},{8,12},{9,13},{10,... | collective-permute-start | bytes 393224 | tf_op jit(solution)/shard_map/ppermute | solution.py:345
  45.2 11.8 %collective-permute-start.4 = (f32[32,1024]{1,0:T(8,128)}, f32[32,1024]{1,0:T(8,128)S(1)}, u32[]{:S(2)}, u32[]{:S(2)}) collective-permute-start(f32[32,1024]{1,0:T(8,128)} %get-tuple-element.26), channel_id=1, source_target_pairs={{0,5},{1,4},{2,7},{3,6},{4,1},{5,0},{6,3},{7,2},{8,13},{9,12},{10,... | collective-permute-start | bytes 393224 | tf_op jit(solution)/shard_map/ppermute | solution.py:345
  45.7 12.1 %collective-permute-start.5 = (f32[32,1024]{1,0:T(8,128)}, f32[32,1024]{1,0:T(8,128)S(1)}, u32[]{:S(2)}, u32[]{:S(2)}) collective-permute-start(f32[32,1024]{1,0:T(8,128)} %get-tuple-element.25), channel_id=1, source_target_pairs={{0,6},{1,7},{2,4},{3,5},{4,2},{5,3},{6,0},{7,1},{8,14},{9,15},{10,... | collective-permute-start | bytes 393224 | tf_op jit(solution)/shard_map/ppermute | solution.py:345
  49.0 11.8 %collective-permute-start.6 = (f32[32,1024]{1,0:T(8,128)S(1)}, f32[32,1024]{1,0:T(8,128)S(1)}, u32[]{:S(2)}, u32[]{:S(2)}) collective-permute-start(f32[32,1024]{1,0:T(8,128)S(1)} %get-tuple-element.24), channel_id=1, source_target_pairs={{0,7},{1,6},{2,5},{3,4},{4,3},{5,2},{6,1},{7,0},{8,15},{9,14},{10,... | collective-permute-start | bytes 393224 | tf_op jit(solution)/shard_map/ppermute | solution.py:345
  62.7 1.4 collective-permute-start.14
  64.1 4.3 %collective-permute-start.15 = (f32[8,640]{1,0:T(8,128)S(1)}, f32[8,640]{1,0:T(8,128)S(1)}, u32[]{:S(2)}, u32[]{:S(2)}) collective-permute-start(f32[8,640]{1,0:T(8,128)S(1)} %get-tuple-element.44), channel_id=1, source_target_pairs={{0,3},{1,2},{2,1},{3,0},{4,7},{5,6},{6,5},{7,4},{8,11},{9,10},{10,... | collective-permute-start | bytes 61448 | tf_op jit(solution)/shard_map/ppermute | solution.py:249
  64.4 5.8 %collective-permute-start.16 = (f32[8,640]{1,0:T(8,128)S(1)}, f32[8,640]{1,0:T(8,128)S(1)}, u32[]{:S(2)}, u32[]{:S(2)}) collective-permute-start(f32[8,640]{1,0:T(8,128)S(1)} %get-tuple-element.46), channel_id=1, source_target_pairs={{0,5},{1,4},{2,7},{3,6},{4,1},{5,0},{6,3},{7,2},{8,13},{9,12},{10,... | collective-permute-start | bytes 61448 | tf_op jit(solution)/shard_map/ppermute | solution.py:249
  68.3 3.8 %collective-permute-start.17 = (f32[8,640]{1,0:T(8,128)S(1)}, f32[8,640]{1,0:T(8,128)S(1)}, u32[]{:S(2)}, u32[]{:S(2)}) collective-permute-start(f32[8,640]{1,0:T(8,128)S(1)} %get-tuple-element.45), channel_id=1, source_target_pairs={{0,6},{1,7},{2,4},{3,5},{4,2},{5,3},{6,0},{7,1},{8,14},{9,15},{10,... | collective-permute-start | bytes 61448 | tf_op jit(solution)/shard_map/ppermute | solution.py:249
  72.2 4.6 %collective-permute-start.18 = (f32[8,640]{1,0:T(8,128)S(1)}, f32[8,640]{1,0:T(8,128)S(1)}, u32[]{:S(2)}, u32[]{:S(2)}) collective-permute-start(f32[8,640]{1,0:T(8,128)S(1)} %add_add_fusion), channel_id=1, source_target_pairs={{0,65},{1,64},{64,1},{65,0},{128,193},{129,192},{192,129},{193,128... | collective-permute-start | bytes 61448 | tf_op jit(solution)/shard_map/ppermute | solution.py:231
  76.8 4.4 %collective-permute-start.19 = (f32[8,640]{1,0:T(8,128)S(1)}, f32[8,640]{1,0:T(8,128)S(1)}, u32[]{:S(2)}, u32[]{:S(2)}) collective-permute-start(f32[8,640]{1,0:T(8,128)S(1)} %add.163), channel_id=1, source_target_pairs={{0,193},{1,192},{64,129},{65,128},{128,65},{129,64},{192,1},{193,0... | collective-permute-start | bytes 61448 | tf_op jit(solution)/shard_map/ppermute | solution.py:231
  81.2 3.4 %collective-permute-start.20 = (f32[8,640]{1,0:T(8,128)S(1)}, f32[8,640]{1,0:T(8,128)S(1)}, u32[]{:S(2)}, u32[]{:S(2)}) collective-permute-start(f32[8,640]{1,0:T(8,128)S(1)} %add.164), channel_id=1, source_target_pairs={{0,9},{1,8},{8,1},{9,0},{16,25},{17,24},{24,17},{25,16},{32,41},{3... | collective-permute-start | bytes 61448 | tf_op jit(solution)/shard_map/ppermute | solution.py:231
  84.6 4.6 %collective-permute-start.21 = (f32[8,640]{1,0:T(8,128)S(1)}, f32[8,640]{1,0:T(8,128)S(1)}, u32[]{:S(2)}, u32[]{:S(2)}) collective-permute-start(f32[8,640]{1,0:T(8,128)S(1)} %add.165), channel_id=1, source_target_pairs={{0,17},{1,16},{8,25},{9,24},{16,1},{17,0},{24,9},{25,8},{32,49},{3... | collective-permute-start | bytes 61448 | tf_op jit(solution)/shard_map/ppermute | solution.py:231
  89.1 7.2 %collective-permute-start.22 = (f32[8,640]{1,0:T(8,128)S(1)}, f32[8,640]{1,0:T(8,128)S(1)}, u32[]{:S(2)}, u32[]{:S(2)}) collective-permute-start(f32[8,640]{1,0:T(8,128)S(1)} %add.166), channel_id=1, source_target_pairs={{0,49},{1,48},{8,57},{9,56},{16,33},{17,32},{24,41},{25,40},{32,17... | collective-permute-start | bytes 61448 | tf_op jit(solution)/shard_map/ppermute | solution.py:231
  96.4 3.8 %collective-permute-start.25 = (f32[8,640]{1,0:T(8,128)S(1)}, f32[8,640]{1,0:T(8,128)S(1)}, u32[]{:S(2)}, u32[]{:S(2)}) collective-permute-start(f32[8,640]{1,0:T(8,128)S(1)} %add.167), channel_id=1, source_target_pairs={{0,3},{1,2},{2,1},{3,0},{4,7},{5,6},{6,5},{7,4},{8,11},{9,10},{10,... | collective-permute-start | bytes 61448 | tf_op jit(solution)/shard_map/ppermute | solution.py:249
  96.4 63.0 %copy-start = (f32[32,32768]{1,0:T(8,128)S(1)}, f32[32,32768]{1,0:T(8,128)}, u32[]{:S(2)}) copy-start(f32[32,32768]{1,0:T(8,128)} %refs_6_.7) | copy-start | bytes 12582916
  96.4 4.2 %collective-permute-start.23 = (f32[8,640]{1,0:T(8,128)S(1)}, f32[8,640]{1,0:T(8,128)S(1)}, u32[]{:S(2)}, u32[]{:S(2)}) collective-permute-start(f32[8,640]{1,0:T(8,128)S(1)} %add.167), channel_id=1, source_target_pairs={{0,6},{1,7},{2,4},{3,5},{4,2},{5,3},{6,0},{7,1},{8,14},{9,15},{10,... | collective-permute-start | bytes 61448 | tf_op jit(solution)/shard_map/ppermute | solution.py:249
  96.5 5.2 %collective-permute-start.24 = (f32[8,640]{1,0:T(8,128)S(1)}, f32[8,640]{1,0:T(8,128)S(1)}, u32[]{:S(2)}, u32[]{:S(2)}) collective-permute-start(f32[8,640]{1,0:T(8,128)S(1)} %add.167), channel_id=1, source_target_pairs={{0,5},{1,4},{2,7},{3,6},{4,1},{5,0},{6,3},{7,2},{8,13},{9,12},{10,... | collective-permute-start | bytes 61448 | tf_op jit(solution)/shard_map/ppermute | solution.py:249
  101.7 1.4 collective-permute-start.26
  112.9 14.6 %collective-permute-start.27 = (f32[64,2048]{1,0:T(8,128)S(1)}, f32[64,2048]{1,0:T(8,128)S(1)}, u32[]{:S(2)}, u32[]{:S(2)}) collective-permute-start(f32[64,2048]{1,0:T(8,128)S(1)} %get-tuple-element.22.refs_1_), channel_id=1, source_target_pairs={{0,2},{2,4},{4,6},{6,0},{1,3},{3,5},{5,7},{7,1},{8,10},{10,12},{12... | collective-permute-start | bytes 1572872 | tf_op jit(solution)/shard_map/ppermute | solution.py:324
  114.0 14.5 %collective-permute-start.29 = (f32[64,2048]{1,0:T(8,128)S(1)}, f32[64,2048]{1,0:T(8,128)S(1)}, u32[]{:S(2)}, u32[]{:S(2)}) collective-permute-start(f32[64,2048]{1,0:T(8,128)S(1)} %get-tuple-element.23.refs_2_), channel_id=1, source_target_pairs={{0,6},{2,0},{4,2},{6,4},{1,7},{3,1},{5,3},{7,5},{8,14},{10,8},{12,... | collective-permute-start | bytes 1572872 | tf_op jit(solution)/shard_map/ppermute | solution.py:324
  115.7 13.5 %collective-permute-start.43 = (f32[64,2048]{1,0:T(8,128)S(1)}, f32[64,2048]{1,0:T(8,128)S(1)}, u32[]{:S(2)}, u32[]{:S(2)}) collective-permute-start(f32[64,2048]{1,0:T(8,128)S(1)} %get-tuple-element.22.refs_1_), channel_id=1, source_target_pairs={{0,1},{1,0},{2,3},{3,2},{4,5},{5,4},{6,7},{7,6},{8,9},{9,8},{10,11... | collective-permute-start | bytes 1572872 | tf_op jit(solution)/shard_map/ppermute | solution.py:328
  116.4 14.9 %collective-permute-start.44 = (f32[64,2048]{1,0:T(8,128)S(1)}, f32[64,2048]{1,0:T(8,128)S(1)}, u32[]{:S(2)}, u32[]{:S(2)}) collective-permute-start(f32[64,2048]{1,0:T(8,128)S(1)} %get-tuple-element.23.refs_2_), channel_id=1, source_target_pairs={{0,1},{1,0},{2,3},{3,2},{4,5},{5,4},{6,7},{7,6},{8,9},{9,8},{10,11... | collective-permute-start | bytes 1572872 | tf_op jit(solution)/shard_map/ppermute | solution.py:328
  116.4 22.4 %collective-permute-start.37 = (f32[64,2048]{1,0:T(8,128)S(1)}, f32[64,2048]{1,0:T(8,128)S(1)}, u32[]{:S(2)}, u32[]{:S(2)}) collective-permute-start(f32[64,2048]{1,0:T(8,128)S(1)} %get-tuple-element.23.refs_2_), channel_id=1, source_target_pairs={{0,2},{2,4},{4,6},{6,0},{1,3},{3,5},{5,7},{7,1},{8,10},{10,12},{12... | collective-permute-start | bytes 1572872 | tf_op jit(solution)/shard_map/ppermute | solution.py:324
  127.6 12.9 %collective-permute-start.38 = (f32[64,2048]{1,0:T(8,128)S(1)}, f32[64,2048]{1,0:T(8,128)S(1)}, u32[]{:S(2)}, u32[]{:S(2)}) collective-permute-start(f32[64,2048]{1,0:T(8,128)S(1)} %get-tuple-element.22.refs_1_), channel_id=1, source_target_pairs={{0,6},{2,0},{4,2},{6,4},{1,7},{3,1},{5,3},{7,5},{8,14},{10,8},{12,... | collective-permute-start | bytes 1572872 | tf_op jit(solution)/shard_map/ppermute | solution.py:324
  128.4 16.0 %collective-permute-start.33 = (f32[64,1024]{1,0:T(8,128)S(1)}, f32[64,1024]{1,0:T(8,128)S(1)}, u32[]{:S(2)}, u32[]{:S(2)}) collective-permute-start(f32[64,1024]{1,0:T(8,128)S(1)} %get-tuple-element.42), channel_id=1, source_target_pairs={{0,2},{2,4},{4,6},{6,0},{1,3},{3,5},{5,7},{7,1},{8,10},{10,12},{12... | collective-permute-start | bytes 786440 | tf_op jit(solution)/shard_map/ppermute | solution.py:324
  129.2 16.8 %collective-permute-start.34 = (f32[64,1024]{1,0:T(8,128)S(1)}, f32[64,1024]{1,0:T(8,128)S(1)}, u32[]{:S(2)}, u32[]{:S(2)}) collective-permute-start(f32[64,1024]{1,0:T(8,128)S(1)} %get-tuple-element.40), channel_id=1, source_target_pairs={{0,6},{2,0},{4,2},{6,4},{1,7},{3,1},{5,3},{7,5},{8,14},{10,8},{12,... | collective-permute-start | bytes 786440 | tf_op jit(solution)/shard_map/ppermute | solution.py:324
  131.3 18.7 %collective-permute-start.28 = (f32[64,1024]{1,0:T(8,128)S(1)}, f32[64,1024]{1,0:T(8,128)S(1)}, u32[]{:S(2)}, u32[]{:S(2)}) collective-permute-start(f32[64,1024]{1,0:T(8,128)S(1)} %get-tuple-element.43), channel_id=1, source_target_pairs={{0,2},{2,4},{4,6},{6,0},{1,3},{3,5},{5,7},{7,1},{8,10},{10,12},{12... | collective-permute-start | bytes 786440 | tf_op jit(solution)/shard_map/ppermute | solution.py:324
  138.8 20.0 %collective-permute-start.41 = (f32[64,2048]{1,0:T(8,128)S(1)}, f32[64,2048]{1,0:T(8,128)S(1)}, u32[]{:S(2)}, u32[]{:S(2)}) collective-permute-start(f32[64,2048]{1,0:T(8,128)S(1)} %collective-permute-done.27.refs_1_), channel_id=1, source_target_pairs={{0,1},{1,0},{2,3},{3,2},{4,5},{5,4},{6,7},{7,6},{8,9},{9,8},{10,11... | collective-permute-start | bytes 1572872 | tf_op jit(solution)/shard_map/ppermute | solution.py:328
  140.4 18.3 %collective-permute-start.42 = (f32[64,2048]{1,0:T(8,128)S(1)}, f32[64,2048]{1,0:T(8,128)S(1)}, u32[]{:S(2)}, u32[]{:S(2)}) collective-permute-start(f32[64,2048]{1,0:T(8,128)S(1)} %collective-permute-done.29.refs_2_), channel_id=1, source_target_pairs={{0,1},{1,0},{2,3},{3,2},{4,5},{5,4},{6,7},{7,6},{8,9},{9,8},{10,11... | collective-permute-start | bytes 1572872 | tf_op jit(solution)/shard_map/ppermute | solution.py:328
  144.4 14.9 %collective-permute-start.39 = (f32[64,2048]{1,0:T(8,128)S(1)}, f32[64,2048]{1,0:T(8,128)S(1)}, u32[]{:S(2)}, u32[]{:S(2)}) collective-permute-start(f32[64,2048]{1,0:T(8,128)S(1)} %collective-permute-done.37.refs_1_), channel_id=1, source_target_pairs={{0,1},{1,0},{2,3},{3,2},{4,5},{5,4},{6,7},{7,6},{8,9},{9,8},{10,11... | collective-permute-start | bytes 1572872 | tf_op jit(solution)/shard_map/ppermute | solution.py:328
  146.0 18.5 %collective-permute-start.40 = (f32[64,2048]{1,0:T(8,128)S(1)}, f32[64,2048]{1,0:T(8,128)S(1)}, u32[]{:S(2)}, u32[]{:S(2)}) collective-permute-start(f32[64,2048]{1,0:T(8,128)S(1)} %collective-permute-done.38.refs_2_), channel_id=1, source_target_pairs={{0,1},{1,0},{2,3},{3,2},{4,5},{5,4},{6,7},{7,6},{8,9},{9,8},{10,11... | collective-permute-start | bytes 1572872 | tf_op jit(solution)/shard_map/ppermute | solution.py:328
  150.0 6.9 %collective-permute-start.30 = (f32[64,1024]{1,0:T(8,128)S(1)}, f32[64,1024]{1,0:T(8,128)S(1)}, u32[]{:S(2)}, u32[]{:S(2)}) collective-permute-start(f32[64,1024]{1,0:T(8,128)S(1)} %get-tuple-element.41), channel_id=1, source_target_pairs={{0,6},{2,0},{4,2},{6,4},{1,7},{3,1},{5,3},{7,5},{8,14},{10,8},{12,... | collective-permute-start | bytes 786440 | tf_op jit(solution)/shard_map/ppermute | solution.py:324
  156.9 10.2 %collective-permute-start.35 = (f32[64,1024]{1,0:T(8,128)S(1)}, f32[64,1024]{1,0:T(8,128)S(1)}, u32[]{:S(2)}, u32[]{:S(2)}) collective-permute-start(f32[64,1024]{1,0:T(8,128)S(1)} %collective-permute-done.33.refs_1_), channel_id=1, source_target_pairs={{0,1},{1,0},{2,3},{3,2},{4,5},{5,4},{6,7},{7,6},{8,9},{9,8},{10,11... | collective-permute-start | bytes 786440 | tf_op jit(solution)/shard_map/ppermute | solution.py:328
  158.8 8.3 %collective-permute-start.36 = (f32[64,1024]{1,0:T(8,128)S(1)}, f32[64,1024]{1,0:T(8,128)S(1)}, u32[]{:S(2)}, u32[]{:S(2)}) collective-permute-start(f32[64,1024]{1,0:T(8,128)S(1)} %collective-permute-done.34.refs_2_), channel_id=1, source_target_pairs={{0,1},{1,0},{2,3},{3,2},{4,5},{5,4},{6,7},{7,6},{8,9},{9,8},{10,11... | collective-permute-start | bytes 786440 | tf_op jit(solution)/shard_map/ppermute | solution.py:328
  158.8 10.6 %collective-permute-start.31 = (f32[64,1024]{1,0:T(8,128)S(1)}, f32[64,1024]{1,0:T(8,128)S(1)}, u32[]{:S(2)}, u32[]{:S(2)}) collective-permute-start(f32[64,1024]{1,0:T(8,128)S(1)} %collective-permute-done.28.refs_1_), channel_id=1, source_target_pairs={{0,1},{1,0},{2,3},{3,2},{4,5},{5,4},{6,7},{7,6},{8,9},{9,8},{10,11... | collective-permute-start | bytes 786440 | tf_op jit(solution)/shard_map/ppermute | solution.py:328
  159.3 10.1 %collective-permute-start.32 = (f32[64,1024]{1,0:T(8,128)S(1)}, f32[64,1024]{1,0:T(8,128)S(1)}, u32[]{:S(2)}, u32[]{:S(2)}) collective-permute-start(f32[64,1024]{1,0:T(8,128)S(1)} %collective-permute-done.30.refs_2_), channel_id=1, source_target_pairs={{0,1},{1,0},{2,3},{3,2},{4,5},{5,4},{6,7},{7,6},{8,9},{9,8},{10,11... | collective-permute-start | bytes 786440 | tf_op jit(solution)/shard_map/ppermute | solution.py:328
  (4 other events, 15.0 us)
